TPU v7x, 256 devices: a whole 4x4x8 slice. The times are simulated.
256 devices in a mesh: ep: 32 (over x, z), tp: 8 (over y, core).
Axes of the slice: x: 4, y: 4, z: 8, core: 2. Of those that a mesh axis runs over, the one named last changes fastest.
Arguments:
- tokens: bfloat16 [8192, 2880], P('ep', 'tp'), may hold values from -6 to 6
- expert_ids: int32 [8192, 4], P('ep'), may hold values from 0 to 63, all different within a row; in each aligned block of 256 rows (0 to 255, 256 to 511, ...) at most 32 rows name the same one
- combine_weights: float32 [8192, 4], P('ep'), may hold values from 0.05 to 0.6
- gate_weight: bfloat16 [64, 2880, 2880], P('ep', None, 'tp'), may hold values from -0.109375 to 0.109375
- up_weight: bfloat16 [64, 2880, 2880], P('ep', None, 'tp'), may hold values from -0.109375 to 0.109375
- down_weight: bfloat16 [64, 2880, 2880], P('ep', 'tp'), may hold values from -0.109375 to 0.109375
Outputs:
- mixed: bfloat16 [8192, 2880], P('ep', 'tp')
Inputs may be any that keep to these rules, and one draw needn't show every extreme that they name: `expert_ids`: each row names 4 different experts; within the 256 rows of one index of ep no expert is named more than 32 times, a bound that some block reaches.
All inputs are finite; a program needn't handle non-finite values.
Results may differ from a plain program's by a relative error of at most 0.014.
Values may be sent and summed in bfloat16 or wider, within the bound.
No kernel may reach another device: no remote copies, remote signals or barrier semaphores. Data moves between devices by JAX's collectives and lax.ppermute only.
A program may use at most 128 MiB of HBM per device.

v0:
```python
import jax
import jax.numpy as jnp
from jax import lax
from jax.experimental import pallas as pl
from jax.experimental.pallas import tpu as pltpu
from jax.sharding import Mesh
from jax.sharding import PartitionSpec as P


PARTS = (16, 16)
CORES = 2
RING = 4
LANES = 384
HALF = 368
GROUP = 32
WIDE = CORES * LANES
VMEM = 56 * 1024 * 1024

f32, bf16 = jnp.float32, jnp.bfloat16
NT = (((1,), (1,)), ((), ()))


def lasting(us):
    return pl.CostEstimate(flops=int(us * 250_000_000), bytes_accessed=0, transcendentals=0)


def slots_of(ids, experts):
    top, toks = ids.shape
    j = lax.broadcasted_iota(jnp.int32, (experts, toks), 0)
    chips = experts // CORES
    named = CORES * lax.rem(j, chips) + lax.div(j, chips)
    hit = [ids[k : k + 1, :] == named for k in range(top)]
    member = sum(h.astype(f32) for h in hit)
    before = lax.broadcasted_iota(jnp.int32, (toks, toks), 0) < lax.broadcasted_iota(jnp.int32, (toks, toks), 1)
    rank = jnp.dot(member.astype(bf16), before.astype(f32).astype(bf16), preferred_element_type=f32)
    return hit, jnp.where(member > 0, rank, -1.0)


def spread(rank, start, size):
    some, toks = rank.shape
    slot = lax.broadcasted_iota(jnp.int32, (some, size, toks), 1).astype(f32) + float(start)
    return jnp.broadcast_to(rank[:, None, :], (some, size, toks)) == slot


def dispatch(ids_t, tok_t, experts, start, size):
    feats, toks = tok_t.shape

    def body(ids_ref, tok_ref, out_ref, pad_ref, rank_ref):
        pad_ref[...] = jnp.zeros(pad_ref.shape, bf16)
        pad_ref[:feats, :] = tok_ref[...]
        rank_ref[...] = slots_of(ids_ref[...], experts)[1]

        @pl.loop(0, experts // GROUP)
        def _(i):
            rank = rank_ref[pl.ds(pl.multiple_of(i * GROUP, GROUP), GROUP), :]
            pick = spread(rank, start, size).astype(f32).reshape(GROUP * size, toks).astype(bf16)
            rows = lax.dot_general(pick, pad_ref[...], NT, preferred_element_type=f32)
            out_ref[pl.ds(pl.multiple_of(i * GROUP * size, GROUP * size), GROUP * size), :] = rows.astype(bf16)

    return pl.pallas_call(
        body,
        out_shape=jax.ShapeDtypeStruct((experts * size, LANES), bf16),
        scratch_shapes=[pltpu.VMEM((LANES, toks), bf16), pltpu.VMEM((experts, toks), f32)],
        compiler_params=pltpu.CompilerParams(vmem_limit_bytes=VMEM),
        cost_estimate=lasting(3),
    )(ids_t, tok_t)


def factors(ids_t, cw_t, experts, start, size):
    toks = ids_t.shape[1]

    def body(ids_ref, cw_ref, high_ref, low_ref, rank_ref, weight_ref):
        hit, rank_ref[...] = slots_of(ids_ref[...], experts)
        cw = cw_ref[...]
        weight_ref[...] = sum(jnp.where(h, cw[k : k + 1, :], 0.0) for k, h in enumerate(hit))

        @pl.loop(0, experts // GROUP)
        def _(i):
            some = pl.ds(pl.multiple_of(i * GROUP, GROUP), GROUP)
            wide = jnp.broadcast_to(weight_ref[some, :][:, None, :], (GROUP, size, toks))
            coef = jnp.where(spread(rank_ref[some, :], start, size), wide, 0.0).reshape(GROUP * size, toks).T
            high = coef.astype(bf16)
            at = pl.ds(pl.multiple_of(i * GROUP * size, GROUP * size), GROUP * size)
            high_ref[:, at] = high
            low_ref[:, at] = (coef - high.astype(f32)).astype(bf16)

    return pl.pallas_call(
        body,
        out_shape=[jax.ShapeDtypeStruct((toks, experts * size), bf16)] * 2,
        scratch_shapes=[pltpu.VMEM((experts, toks), f32)] * 2,
        compiler_params=pltpu.CompilerParams(vmem_limit_bytes=VMEM),
        cost_estimate=lasting(4),
    )(ids_t, cw_t)


def combine(rows, parts, acc, feats):
    toks = parts[0].shape[0]
    last = feats is not None

    def body(rows_ref, high_ref, low_ref, *refs):
        out_ref = refs[-1]
        total = jnp.dot(high_ref[...], rows_ref[...], preferred_element_type=f32)
        total += jnp.dot(low_ref[...], rows_ref[...], preferred_element_type=f32)
        if acc is not None:
            total += refs[0][...]
        out_ref[...] = total.T[:feats, :].astype(bf16) if last else total

    return pl.pallas_call(
        body,
        out_shape=jax.ShapeDtypeStruct((feats, toks), bf16) if last else jax.ShapeDtypeStruct((toks, LANES), f32),
        compiler_params=pltpu.CompilerParams(vmem_limit_bytes=VMEM),
        cost_estimate=lasting(2),
        name="combine",
    )(rows, *parts, *(() if acc is None else (acc,)))


def arrange(core, own, received):
    _, units, width = own.shape
    feats = width // (RING * CORES)

    def body(core_ref, own_ref, recv_ref, out_ref):
        for first in (0, HALF):
            out_ref[0, first + units : first + HALF, :] = jnp.zeros((HALF - units, WIDE), bf16)
        for c in range(CORES):
            out_ref[0, :, c * LANES + feats : (c + 1) * LANES] = jnp.zeros((2 * HALF, LANES - feats), bf16)
        for q in range(RING):

            @pl.when(pl.program_id(0) == q)
            def _(q=q):
                for c in range(CORES):
                    j = (CORES * q + c) * feats
                    to = slice(c * LANES, c * LANES + feats)
                    out_ref[0, :units, to] = own_ref[0, :, j : j + feats]
                    out_ref[0, HALF : HALF + units, to] = recv_ref[:, j : j + feats]

    return pl.pallas_call(
        body,
        grid_spec=pltpu.PrefetchScalarGridSpec(
            num_scalar_prefetch=1,
            grid=(RING,),
            in_specs=[
                pl.BlockSpec((1, units, width), lambda i, c: (c[0], 0, 0)),
                pl.BlockSpec((units, width), lambda i, c: (0, 0)),
            ],
            out_specs=pl.BlockSpec((1, 2 * HALF, WIDE), lambda i, c: (i, 0, 0)),
        ),
        out_shape=jax.ShapeDtypeStruct((RING, 2 * HALF, WIDE), bf16),
        compiler_params=pltpu.CompilerParams(vmem_limit_bytes=VMEM),
        cost_estimate=lasting(6),
        name="arrange",
    )(core, own, received)


CAME = [((0, 0), (0, 1)), ((1, 0), (1, 1)), ((3, 0), (3, 1)), ((2, 0),), ((2, 1),)]
GOES = [((0, 0), (0, 1)), ((2, 0), (1, 1)), ((2, 1), (3, 0)), ((1, 0),), ((3, 1),)]


def copies(row, arrays, keys, buf, sem, out, only=None):
    for i, (ref, blocks) in enumerate(zip(arrays, keys)):
        for b, (k, c) in enumerate(blocks):
            if only is None or only == k:
                here = buf.at[lax.rem(row + k, RING), :, pl.ds(c * LANES, LANES)]
                ends = (here, ref.at[b]) if out else (ref.at[b], here)
                yield pltpu.make_async_copy(*ends, sem.at[i, b])


def kernel(body, inputs, out_shape, scratch, us):
    hbm = pl.BlockSpec(memory_space=pltpu.MemorySpace.HBM)
    many = isinstance(out_shape, list)
    return pl.pallas_call(
        body,
        in_specs=[pl.BlockSpec(memory_space=pltpu.MemorySpace.SMEM)] + [hbm] * (len(inputs) - 1),
        out_specs=[hbm] * len(out_shape) if many else pl.BlockSpec(memory_space=pltpu.MemorySpace.VMEM),
        out_shape=out_shape,
        scratch_shapes=scratch,
        compiler_params=pltpu.CompilerParams(vmem_limit_bytes=VMEM),
        cost_estimate=lasting(us),
    )(*inputs)


def lift(row, pieces, gate_w, up_w):
    h = pieces[0].shape[1]
    units = gate_w.shape[1]

    def body(row_ref, *refs):
        xs, ws, out_ref = refs[:5], refs[5:7], refs[7]
        x, g, u, gate, up, xsem, wsem = refs[8:]
        row = row_ref[0]

        def load(w, k):
            j = lax.rem(row + k, RING)
            return pltpu.make_async_copy(ws[w].at[j], (g, u)[w].at[j], wsem.at[w, k])

        for k in range(RING):
            for cp in copies(row, xs, CAME, x, xsem, False, k):
                cp.start()
            load(0, k).start()
            load(1, k).start()
        gate[...] = jnp.zeros(gate.shape, f32)
        up[...] = jnp.zeros(up.shape, f32)

        @pl.loop(0, RING)
        def _(k):
            j = lax.rem(row + k, RING)
            for some in range(RING):

                @pl.when(k == some)
                def _(some=some):
                    for cp in copies(row, xs, CAME, x, xsem, False, some):
                        cp.wait()

            load(0, k).wait()
            gate[...] += lax.dot_general(x[j], g[j], NT, preferred_element_type=f32)
            load(1, k).wait()
            up[...] += lax.dot_general(x[j], u[j], NT, preferred_element_type=f32)

        a = gate[...]
        out_ref[...] = ((up[...] + 1.0) * a * jax.nn.sigmoid(1.702 * a)).astype(bf16)

    return kernel(
        body,
        (row, *pieces, gate_w, up_w),
        jax.ShapeDtypeStruct((h, units), bf16),
        [pltpu.VMEM((RING, h, WIDE), bf16)]
        + [pltpu.VMEM(gate_w.shape, bf16)] * 2
        + [pltpu.VMEM((h, units), f32)] * 2
        + [pltpu.SemaphoreType.DMA((5, 2)), pltpu.SemaphoreType.DMA((2, RING))],
        9 * h // 512,
    )


def lower(row, hidden, down_w):
    h = hidden.shape[0]

    def body(row_ref, hid_ref, w_ref, *refs):
        outs = refs[:5]
        hid, d, y, hsem, wsem, ysem = refs[5:]
        row = row_ref[0]
        fetch = pltpu.make_async_copy(hid_ref, hid, hsem)
        fetch.start()

        def load(k):
            j = lax.rem(row + k, RING)
            return pltpu.make_async_copy(w_ref.at[j], d.at[j], wsem.at[k])

        for k in range(RING):
            load(RING - 1 - k).start()
        fetch.wait()

        @pl.loop(0, RING)
        def _(i):
            k = RING - 1 - i
            j = lax.rem(row + k, RING)
            load(k).wait()
            y[j] = jnp.dot(hid[...], d[j], preferred_element_type=f32).astype(bf16)
            for some in range(RING):

                @pl.when(k == some)
                def _(some=some):
                    for cp in copies(row, outs, GOES, y, ysem, True, some):
                        cp.start()

        for cp in copies(row, outs, GOES, y, ysem, True):
            cp.wait()

    return kernel(
        body,
        (row, hidden, down_w),
        [jax.ShapeDtypeStruct((len(k), h, LANES), bf16) for k in GOES],
        [pltpu.VMEM(hidden.shape, bf16), pltpu.VMEM(down_w.shape, bf16), pltpu.VMEM((RING, h, WIDE), bf16)]
        + [pltpu.SemaphoreType.DMA, pltpu.SemaphoreType.DMA((RING,)), pltpu.SemaphoreType.DMA((5, 2))],
        5 * h // 512,
    )


def shift(array, by):
    return lax.ppermute(array, "y", [(i, (i + by) % RING) for i in range(RING)])


def gathered(own):
    own = own.reshape(CORES, -1, LANES)
    back, fore = shift(own, 1), shift(own, -1)
    far_a, far_b = shift(back[:1], 1), shift(fore[1:], -1)
    return own, fore, back, far_a, far_b


def added(*parts):
    return sum(p.astype(f32) for p in parts).astype(bf16)


def scattered(parts):
    own, plus, minus, later_a, later_b = parts
    plus, minus = shift(plus, 1), shift(minus, -1)
    back_a = shift(added(later_a, plus[:1]), 1)
    fore_b = shift(added(later_b, minus[:1]), -1)
    total = jnp.concatenate([added(own[:1], minus[1:], back_a), added(own[1:], plus[1:], fore_b)])
    return total.reshape(-1, LANES)


def exchange(array):
    return lax.all_to_all(array, ("c", "x", "z"), 0, 0, tiled=True)


def local(tokens, expert_ids, combine_weights, gate_weight, up_weight, down_weight):
    experts = gate_weight.shape[0] * lax.axis_size(("x", "z"))
    feats = tokens.shape[1]
    core = lax.axis_index("c").astype(jnp.int32)
    row = lax.axis_index("y").astype(jnp.int32)[None]
    tok_t, ids_t, cw_t = tokens.T, expert_ids.T, combine_weights.T

    arranged = []
    for w in (gate_weight.swapaxes(1, 2), up_weight.swapaxes(1, 2), down_weight):
        other = lax.dynamic_index_in_dim(w, 1 - core, 0, keepdims=False)
        other = lax.ppermute(other, "c", [(0, 1), (1, 0)])
        arranged.append(arrange(core[None], w, other))

    returned, parts = [], []
    for i, size in enumerate(PARTS):
        start = sum(PARTS[:i])
        sent = dispatch(ids_t, tok_t, experts, start, size)
        sent = exchange(sent)
        pieces = gathered(sent)
        hidden = lift(row, pieces, *arranged[:2])
        part = lower(row, hidden, arranged[2])
        part = scattered(part)
        returned.append(exchange(part))
        parts.append(factors(ids_t, cw_t, experts, start, size))
    acc = None
    for i in range(len(PARTS)):
        acc = combine(returned[i], parts[i], acc, feats if i == len(PARTS) - 1 else None)
    return acc.T


def solution(mesh):
    split = Mesh(mesh.devices.reshape(4, -1, RING, CORES), ("x", "z", "y", "c"))
    ep, tp = ("x", "z"), ("y", "c")
    placed = (P(ep, tp), P(ep, None), P(ep, None), P(ep, None, tp), P(ep, None, tp), P(ep, tp, None))

    return jax.shard_map(local, mesh=split, in_specs=placed, out_specs=P(ep, tp), check_vma=False)
```

profile of v0, /device:TPU:32, one launch (start us, length us, event | category | flops | bytes accessed | tf_op | source)
XLA Modules:
  0.0 232.4 jit_solution(903332754258446343)
XLA Ops:
  2.6 11.6 %all-to-all-start.2 = ((bf16[64,16,384]{2,1,0:T(8,128)(2,1)}), bf16[64,16,384]{2,1,0:T(8,128)(2,1)S(1)}, u32[]{:S(2)}, u32[]{:S(2)}) async-start(bf16[64,16,384]{2,1,0:T(8,128)(2,1)} %bitcast.36), calls=%async_computation.2 | async-start | bytes 1572864 | tf_op jit(solution)/shard_map/all_to_all | solution.py:301
  14.3 3.3 %dynamic-slice_bitcast_fusion.2 = bf16[360,2880]{1,0:T(8,128)(2,1)} fusion(bf16[2,2880,360]{1,2,0:T(8,128)(2,1)} %param.9, s32[]{:T(128)S(6)} %select_n.6), kind=kLoop, calls=%fused_computation.2 | loop fusion | bytes 4147204 | tf_op jit(solution)/shard_map/jit(dynamic_index_in_dim)/squeeze | solution.py:313
  24.0 15.0 %all-to-all-done.2 = bf16[64,16,384]{2,1,0:T(8,128)(2,1)S(1)} async-done(((bf16[64,16,384]{2,1,0:T(8,128)(2,1)}), bf16[64,16,384]{2,1,0:T(8,128)(2,1)S(1)}, u32[]{:S(2)}, u32[]{:S(2)}) %all-to-all-start.2) | async-done | bytes 786464 | tf_op jit(solution)/shard_map/all_to_all | solution.py:301
  39.0 4.6 %all-to-all-start = ((bf16[64,16,384]{2,1,0:T(8,128)(2,1)}), bf16[64,16,384]{2,1,0:T(8,128)(2,1)S(1)}, u32[]{:S(2)}, u32[]{:S(2)}) async-start(bf16[64,16,384]{2,1,0:T(8,128)(2,1)} %bitcast.37), calls=%async_computation | async-start | bytes 1572864 | tf_op jit(solution)/shard_map/all_to_all | solution.py:301
  46.9 21.6 %all-to-all-done = bf16[64,16,384]{2,1,0:T(8,128)(2,1)S(1)} async-done(((bf16[64,16,384]{2,1,0:T(8,128)(2,1)}), bf16[64,16,384]{2,1,0:T(8,128)(2,1)S(1)}, u32[]{:S(2)}, u32[]{:S(2)}) %all-to-all-start) | async-done | bytes 786464 | tf_op jit(solution)/shard_map/all_to_all | solution.py:301
  73.7 5.6 %arrange.5.w_ref = bf16[4,736,768]{2,1,0:T(8,128)(2,1)} custom-call(s32[1]{0:T(128)} %bitcast.5.core_ref, bf16[2,360,2880]{2,1,0:T(8,128)(2,1)} %own_ref.1, bf16[360,2880]{1,0:T(8,128)(2,1)} %collective-permute-done.6.recv_ref), custom_call_target="tpu_custom_call" | custom-call | flops 1500000000 | tf_op jit(solution)/shard_map/arrange/pallas_call | solution.py:136
  80.0 5.7 %arrange.3.refs_5_ = bf16[4,736,768]{2,1,0:T(8,128)(2,1)} custom-call(s32[1]{0:T(128)} %bitcast.5.core_ref, bf16[2,360,2880]{2,1,0:T(8,128)(2,1)} %bitcast.26, bf16[360,2880]{1,0:T(8,128)(2,1)} %collective-permute-done.4.recv_ref), custom_call_target="tpu_custom_call" | custom-call | flops 1500000000 | tf_op jit(solution)/shard_map/arrange/pallas_call | solution.py:136
  85.7 5.6 %arrange.4.refs_6_ = bf16[4,736,768]{2,1,0:T(8,128)(2,1)} custom-call(s32[1]{0:T(128)} %bitcast.5.core_ref, bf16[2,360,2880]{2,1,0:T(8,128)(2,1)} %bitcast.27, bf16[360,2880]{1,0:T(8,128)(2,1)} %collective-permute-done.5.recv_ref), custom_call_target="tpu_custom_call" | custom-call | flops 1500000000 | tf_op jit(solution)/shard_map/arrange/pallas_call | solution.py:136
  91.2 5.8 %collective-permute-done.13.refs_3_ = bf16[1,512,384]{2,1,0:T(8,128)(2,1)S(1)} collective-permute-done((bf16[1,512,384]{2,1,0:T(8,128)(2,1)S(1)}, bf16[1,512,384]{2,1,0:T(8,128)(2,1)S(1)}, u32[]{:S(2)}, u32[]{:S(2)}) %collective-permute-start.13) | collective-permute-done | bytes 393248 | tf_op jit(solution)/shard_map/ppermute | solution.py:277
  98.0 10.9 %shard_map.69.hid_ref = bf16[512,736]{1,0:T(8,128)(2,1)} custom-call(s32[1]{0:T(128)} %bitcast.row_ref, bf16[2,512,384]{2,1,0:T(8,128)(2,1)} %bitcast.33, bf16[2,512,384]{2,1,0:T(8,128)(2,1)} %copy-done.9, bf16[2,512,384]{2,1,0:T(8,128)(2,1)} %copy-done.8, bf16[1,512,384]{2,1,0:T(8,128)(2,1)} %copy-done.13, bf16[1,512,384]{2,1,0:T(8,128)(2,1)} %copy-done.15, ...), custom_call_target="tpu_custom_call" | custom-call | flops 2249999872 | tf_op jit(solution)/shard_map/pallas_call | solution.py:170
  108.8 6.0 %shard_map.70 = (bf16[2,512,384]{2,1,0:T(8,128)(2,1)}, bf16[2,512,384]{2,1,0:T(8,128)(2,1)}, bf16[2,512,384]{2,1,0:T(8,128)(2,1)}, bf16[1,512,384]{2,1,0:T(8,128)(2,1)}, bf16[1,512,384]{2,1,0:T(8,128)(2,1)}) custom-call(s32[1]{0:T(128)} %bitcast.row_ref, bf16[512,736]{1,0:T(8,128)(2,1)} %shard_map.69.hid_ref, bf16[4,736,768]{2,1,0:T(8,128)(2,1)} %arrange.5.w_ref), custom_call_target="tpu_custom_call" | custom-call | flops 1250000000 | tf_op jit(solution)/shard_map/pallas_call | solution.py:170
  117.5 3.0 %collective-permute-start.3 = (bf16[1,512,384]{2,1,0:T(8,128)(2,1)S(1)}, bf16[1,512,384]{2,1,0:T(8,128)(2,1)S(1)}, u32[]{:S(2)}, u32[]{:S(2)}) collective-permute-start(bf16[1,512,384]{2,1,0:T(8,128)(2,1)S(1)} %slice.65), channel_id=1, source_target_pairs={{0,6},{2,0},{4,2},{6,4},{1,7},{3,1},{5,3},{7,5},{8,14},{10,8},{12,... | collective-permute-start | bytes 1179656 | tf_op jit(solution)/shard_map/ppermute | solution.py:277
  120.5 15.1 %collective-permute-done.15 = bf16[2,512,384]{2,1,0:T(8,128)(2,1)S(1)} collective-permute-done((bf16[2,512,384]{2,1,0:T(8,128)(2,1)}, bf16[2,512,384]{2,1,0:T(8,128)(2,1)S(1)}, u32[]{:S(2)}, u32[]{:S(2)}) %collective-permute-start.15) | collective-permute-done | bytes 786464 | tf_op jit(solution)/shard_map/ppermute | solution.py:277
  136.7 3.0 %collective-permute-start.18 = (bf16[1,512,384]{2,1,0:T(8,128)(2,1)S(1)}, bf16[1,512,384]{2,1,0:T(8,128)(2,1)S(1)}, u32[]{:S(2)}, u32[]{:S(2)}) collective-permute-start(bf16[1,512,384]{2,1,0:T(8,128)(2,1)S(1)} %add_convert_fusion.1), channel_id=1, source_target_pairs={{0,6},{2,0},{4,2},{6,4},{1,7},{3,1},{5,3},{7,5},{8,14},{10,8},{12,... | collective-permute-start | bytes 1179656 | tf_op jit(solution)/shard_map/ppermute | solution.py:277
  141.1 5.8 %collective-permute-done.2.refs_3_ = bf16[1,512,384]{2,1,0:T(8,128)(2,1)S(1)} collective-permute-done((bf16[1,512,384]{2,1,0:T(8,128)(2,1)S(1)}, bf16[1,512,384]{2,1,0:T(8,128)(2,1)S(1)}, u32[]{:S(2)}, u32[]{:S(2)}) %collective-permute-start.2) | collective-permute-done | bytes 393248 | tf_op jit(solution)/shard_map/ppermute | solution.py:277
  148.5 10.9 %shard_map.65.hid_ref = bf16[512,736]{1,0:T(8,128)(2,1)} custom-call(s32[1]{0:T(128)} %bitcast.row_ref, bf16[2,512,384]{2,1,0:T(8,128)(2,1)} %bitcast.30, bf16[2,512,384]{2,1,0:T(8,128)(2,1)} %copy-done.7, bf16[2,512,384]{2,1,0:T(8,128)(2,1)} %copy-done.6, bf16[1,512,384]{2,1,0:T(8,128)(2,1)} %copy-done.12, bf16[1,512,384]{2,1,0:T(8,128)(2,1)} %copy-done.14, ...), custom_call_target="tpu_custom_call" | custom-call | flops 2249999872 | tf_op jit(solution)/shard_map/pallas_call | solution.py:170
  159.3 6.1 %shard_map.66 = (bf16[2,512,384]{2,1,0:T(8,128)(2,1)}, bf16[2,512,384]{2,1,0:T(8,128)(2,1)}, bf16[2,512,384]{2,1,0:T(8,128)(2,1)}, bf16[1,512,384]{2,1,0:T(8,128)(2,1)}, bf16[1,512,384]{2,1,0:T(8,128)(2,1)}) custom-call(s32[1]{0:T(128)} %bitcast.row_ref, bf16[512,736]{1,0:T(8,128)(2,1)} %shard_map.65.hid_ref, bf16[4,736,768]{2,1,0:T(8,128)(2,1)} %arrange.5.w_ref), custom_call_target="tpu_custom_call" | custom-call | flops 1250000000 | tf_op jit(solution)/shard_map/pallas_call | solution.py:170
  168.9 5.3 %all-to-all-start.3 = ((bf16[64,16,384]{2,1,0:T(8,128)(2,1)}), bf16[64,16,384]{2,1,0:T(8,128)(2,1)S(1)}, u32[]{:S(2)}, u32[]{:S(2)}) async-start(bf16[64,16,384]{2,1,0:T(8,128)(2,1)} %bitcast.18), calls=%async_computation.3 | async-start | bytes 1572864 | tf_op jit(solution)/shard_map/all_to_all | solution.py:301
  174.2 7.1 %collective-permute-done.7 = bf16[2,512,384]{2,1,0:T(8,128)(2,1)S(1)} collective-permute-done((bf16[2,512,384]{2,1,0:T(8,128)(2,1)}, bf16[2,512,384]{2,1,0:T(8,128)(2,1)S(1)}, u32[]{:S(2)}, u32[]{:S(2)}) %collective-permute-start.7) | collective-permute-done | bytes 786464 | tf_op jit(solution)/shard_map/ppermute | solution.py:277
  184.7 5.6 %collective-permute-done.10 = bf16[1,512,384]{2,1,0:T(8,128)(2,1)S(1)} collective-permute-done((bf16[1,512,384]{2,1,0:T(8,128)(2,1)S(1)}, bf16[1,512,384]{2,1,0:T(8,128)(2,1)S(1)}, u32[]{:S(2)}, u32[]{:S(2)}) %collective-permute-start.10) | collective-permute-done | bytes 393248 | tf_op jit(solution)/shard_map/ppermute | solution.py:277
  193.5 5.5 %all-to-all-done.3 = bf16[64,16,384]{2,1,0:T(8,128)(2,1)S(1)} async-done(((bf16[64,16,384]{2,1,0:T(8,128)(2,1)}), bf16[64,16,384]{2,1,0:T(8,128)(2,1)S(1)}, u32[]{:S(2)}, u32[]{:S(2)}) %all-to-all-start.3) | async-done | bytes 786464 | tf_op jit(solution)/shard_map/all_to_all | solution.py:301
  199.0 4.6 %all-to-all-start.1 = ((bf16[64,16,384]{2,1,0:T(8,128)(2,1)}), bf16[64,16,384]{2,1,0:T(8,128)(2,1)S(1)}, u32[]{:S(2)}, u32[]{:S(2)}) async-start(bf16[64,16,384]{2,1,0:T(8,128)(2,1)} %bitcast.13), calls=%async_computation.1 | async-start | bytes 1572864 | tf_op jit(solution)/shard_map/all_to_all | solution.py:301
  211.1 17.4 %all-to-all-done.1 = bf16[64,16,384]{2,1,0:T(8,128)(2,1)S(1)} async-done(((bf16[64,16,384]{2,1,0:T(8,128)(2,1)}), bf16[64,16,384]{2,1,0:T(8,128)(2,1)S(1)}, u32[]{:S(2)}, u32[]{:S(2)}) %all-to-all-start.1) | async-done | bytes 786464 | tf_op jit(solution)/shard_map/all_to_all | solution.py:301
  229.4 3.0 %combine.3 = bf16[360,256]{1,0:T(8,128)(2,1)} custom-call(bf16[1024,384]{1,0:T(8,128)(2,1)} %bitcast.35, bf16[256,1024]{1,0:T(8,128)(2,1)} %get-tuple-element.24.high_ref, bf16[256,1024]{1,0:T(8,128)(2,1)} %get-tuple-element.25.low_ref, f32[256,384]{1,0:T(8,128)} %combine.2.refs_0_), custom_call_target="tpu_custom_call" | custom-call | flops 500000000 | tf_op jit(solution)/shard_map/combine/pallas_call | solution.py:108
  (84 shorter events, 44.1 us)
Async XLA Ops:
  2.6 36.4 %all-to-all-start.2 = ((bf16[64,16,384]{2,1,0:T(8,128)(2,1)}), bf16[64,16,384]{2,1,0:T(8,128)(2,1)S(1)}, u32[]{:S(2)}, u32[]{:S(2)}) async-start(bf16[64,16,384]{2,1,0:T(8,128)(2,1)} %bitcast.36), calls=%async_computation.2 | async-start | bytes 1572864 | tf_op jit(solution)/shard_map/all_to_all | solution.py:301
  17.6 61.7 %collective-permute-start.4 = (bf16[360,2880]{1,0:T(8,128)(2,1)}, bf16[360,2880]{1,0:T(8,128)(2,1)}, u32[]{:S(2)}, u32[]{:S(2)}) collective-permute-start(bf16[360,2880]{1,0:T(8,128)(2,1)} %dynamic-slice_bitcast_fusion.2), channel_id=1, source_target_pairs={{0,1},{1,0},{2,3},{3,2},{4,5},{5,4},{6,7},{7,6},{8,9},{9,8},{10,11... | collective-permute-start | bytes 6220808 | tf_op jit(solution)/shard_map/ppermute | solution.py:314
  19.4 52.6 %collective-permute-start.6 = (bf16[360,2880]{1,0:T(8,128)(2,1)}, bf16[360,2880]{1,0:T(8,128)(2,1)}, u32[]{:S(2)}, u32[]{:S(2)}) collective-permute-start(bf16[360,2880]{1,0:T(8,128)(2,1)} %dynamic-slice_bitcast_fusion), channel_id=1, source_target_pairs={{0,1},{1,0},{2,3},{3,2},{4,5},{5,4},{6,7},{7,6},{8,9},{9,8},{10,11... | collective-permute-start | bytes 6220808 | tf_op jit(solution)/shard_map/ppermute | solution.py:314
  21.2 64.5 %collective-permute-start.5 = (bf16[360,2880]{1,0:T(8,128)(2,1)}, bf16[360,2880]{1,0:T(8,128)(2,1)}, u32[]{:S(2)}, u32[]{:S(2)}) collective-permute-start(bf16[360,2880]{1,0:T(8,128)(2,1)} %dynamic-slice_bitcast_fusion.1), channel_id=1, source_target_pairs={{0,1},{1,0},{2,3},{3,2},{4,5},{5,4},{6,7},{7,6},{8,9},{9,8},{10,11... | collective-permute-start | bytes 6220808 | tf_op jit(solution)/shard_map/ppermute | solution.py:314
  39.0 40.2 %copy-start.3 = (bf16[64,16,384]{2,1,0:T(8,128)(2,1)}, bf16[64,16,384]{2,1,0:T(8,128)(2,1)S(1)}, u32[]{:S(2)}) copy-start(bf16[64,16,384]{2,1,0:T(8,128)(2,1)S(1)} %all-to-all-done.2) | copy-start | bytes 2359300
  39.0 29.5 %all-to-all-start = ((bf16[64,16,384]{2,1,0:T(8,128)(2,1)}), bf16[64,16,384]{2,1,0:T(8,128)(2,1)S(1)}, u32[]{:S(2)}, u32[]{:S(2)}) async-start(bf16[64,16,384]{2,1,0:T(8,128)(2,1)} %bitcast.37), calls=%async_computation | async-start | bytes 1572864 | tf_op jit(solution)/shard_map/all_to_all | solution.py:301
  43.6 24.9 %collective-permute-start.12 = (bf16[2,512,384]{2,1,0:T(8,128)(2,1)S(1)}, bf16[2,512,384]{2,1,0:T(8,128)(2,1)S(1)}, u32[]{:S(2)}, u32[]{:S(2)}) collective-permute-start(bf16[2,512,384]{2,1,0:T(8,128)(2,1)S(1)} %bitcast.31), channel_id=1, source_target_pairs={{0,2},{2,4},{4,6},{6,0},{1,3},{3,5},{5,7},{7,1},{8,10},{10,12},{12... | collective-permute-start | bytes 2359304 | tf_op jit(solution)/shard_map/ppermute | solution.py:277
  45.3 24.9 %collective-permute-start.11 = (bf16[2,512,384]{2,1,0:T(8,128)(2,1)S(1)}, bf16[2,512,384]{2,1,0:T(8,128)(2,1)S(1)}, u32[]{:S(2)}, u32[]{:S(2)}) collective-permute-start(bf16[2,512,384]{2,1,0:T(8,128)(2,1)S(1)} %bitcast.32), channel_id=1, source_target_pairs={{0,6},{2,0},{4,2},{6,4},{1,7},{3,1},{5,3},{7,5},{8,14},{10,8},{12,... | collective-permute-start | bytes 2359304 | tf_op jit(solution)/shard_map/ppermute | solution.py:277
  68.5 48.5 %collective-permute-start.1 = (bf16[2,512,384]{2,1,0:T(8,128)(2,1)S(1)}, bf16[2,512,384]{2,1,0:T(8,128)(2,1)S(1)}, u32[]{:S(2)}, u32[]{:S(2)}) collective-permute-start(bf16[2,512,384]{2,1,0:T(8,128)(2,1)S(1)} %bitcast.28), channel_id=1, source_target_pairs={{0,2},{2,4},{4,6},{6,0},{1,3},{3,5},{5,7},{7,1},{8,10},{10,12},{12... | collective-permute-start | bytes 2359304 | tf_op jit(solution)/shard_map/ppermute | solution.py:277
  70.2 26.8 %collective-permute-start.13 = (bf16[1,512,384]{2,1,0:T(8,128)(2,1)S(1)}, bf16[1,512,384]{2,1,0:T(8,128)(2,1)S(1)}, u32[]{:S(2)}, u32[]{:S(2)}) collective-permute-start(bf16[1,512,384]{2,1,0:T(8,128)(2,1)S(1)} %slice.70), channel_id=1, source_target_pairs={{0,2},{2,4},{4,6},{6,0},{1,3},{3,5},{5,7},{7,1},{8,10},{10,12},{12... | collective-permute-start | bytes 1179656 | tf_op jit(solution)/shard_map/ppermute | solution.py:277
  71.9 25.1 %collective-permute-start.14 = (bf16[1,512,384]{2,1,0:T(8,128)(2,1)S(1)}, bf16[1,512,384]{2,1,0:T(8,128)(2,1)S(1)}, u32[]{:S(2)}, u32[]{:S(2)}) collective-permute-start(bf16[1,512,384]{2,1,0:T(8,128)(2,1)S(1)} %slice.71), channel_id=1, source_target_pairs={{0,6},{2,0},{4,2},{6,4},{1,7},{3,1},{5,3},{7,5},{8,14},{10,8},{12,... | collective-permute-start | bytes 1179656 | tf_op jit(solution)/shard_map/ppermute | solution.py:277
  79.3 38.1 %collective-permute-start = (bf16[2,512,384]{2,1,0:T(8,128)(2,1)S(1)}, bf16[2,512,384]{2,1,0:T(8,128)(2,1)S(1)}, u32[]{:S(2)}, u32[]{:S(2)}) collective-permute-start(bf16[2,512,384]{2,1,0:T(8,128)(2,1)S(1)} %bitcast.29), channel_id=1, source_target_pairs={{0,6},{2,0},{4,2},{6,4},{1,7},{3,1},{5,3},{7,5},{8,14},{10,8},{12,... | collective-permute-start | bytes 2359304 | tf_op jit(solution)/shard_map/ppermute | solution.py:277
  114.9 20.7 %collective-permute-start.15 = (bf16[2,512,384]{2,1,0:T(8,128)(2,1)}, bf16[2,512,384]{2,1,0:T(8,128)(2,1)S(1)}, u32[]{:S(2)}, u32[]{:S(2)}) collective-permute-start(bf16[2,512,384]{2,1,0:T(8,128)(2,1)} %get-tuple-element.27), channel_id=1, source_target_pairs={{0,6},{2,0},{4,2},{6,4},{1,7},{3,1},{5,3},{7,5},{8,14},{10,8},{12,... | collective-permute-start | bytes 2359304 | tf_op jit(solution)/shard_map/ppermute | solution.py:277
  116.7 23.0 %collective-permute-start.16 = (bf16[2,512,384]{2,1,0:T(8,128)(2,1)}, bf16[2,512,384]{2,1,0:T(8,128)(2,1)S(1)}, u32[]{:S(2)}, u32[]{:S(2)}) collective-permute-start(bf16[2,512,384]{2,1,0:T(8,128)(2,1)} %get-tuple-element.29), channel_id=1, source_target_pairs={{0,2},{2,4},{4,6},{6,0},{1,3},{3,5},{5,7},{7,1},{8,10},{10,12},{12... | collective-permute-start | bytes 2359304 | tf_op jit(solution)/shard_map/ppermute | solution.py:277
  117.0 29.9 %collective-permute-start.2 = (bf16[1,512,384]{2,1,0:T(8,128)(2,1)S(1)}, bf16[1,512,384]{2,1,0:T(8,128)(2,1)S(1)}, u32[]{:S(2)}, u32[]{:S(2)}) collective-permute-start(bf16[1,512,384]{2,1,0:T(8,128)(2,1)S(1)} %slice.64), channel_id=1, source_target_pairs={{0,2},{2,4},{4,6},{6,0},{1,3},{3,5},{5,7},{7,1},{8,10},{10,12},{12... | collective-permute-start | bytes 1179656 | tf_op jit(solution)/shard_map/ppermute | solution.py:277
  117.5 29.5 %collective-permute-start.3 = (bf16[1,512,384]{2,1,0:T(8,128)(2,1)S(1)}, bf16[1,512,384]{2,1,0:T(8,128)(2,1)S(1)}, u32[]{:S(2)}, u32[]{:S(2)}) collective-permute-start(bf16[1,512,384]{2,1,0:T(8,128)(2,1)S(1)} %slice.65), channel_id=1, source_target_pairs={{0,6},{2,0},{4,2},{6,4},{1,7},{3,1},{5,3},{7,5},{8,14},{10,8},{12,... | collective-permute-start | bytes 1179656 | tf_op jit(solution)/shard_map/ppermute | solution.py:277
  136.7 30.9 %collective-permute-start.18 = (bf16[1,512,384]{2,1,0:T(8,128)(2,1)S(1)}, bf16[1,512,384]{2,1,0:T(8,128)(2,1)S(1)}, u32[]{:S(2)}, u32[]{:S(2)}) collective-permute-start(bf16[1,512,384]{2,1,0:T(8,128)(2,1)S(1)} %add_convert_fusion.1), channel_id=1, source_target_pairs={{0,6},{2,0},{4,2},{6,4},{1,7},{3,1},{5,3},{7,5},{8,14},{10,8},{12,... | collective-permute-start | bytes 1179656 | tf_op jit(solution)/shard_map/ppermute | solution.py:277
  140.8 26.8 %collective-permute-start.17 = (bf16[1,512,384]{2,1,0:T(8,128)(2,1)S(1)}, bf16[1,512,384]{2,1,0:T(8,128)(2,1)S(1)}, u32[]{:S(2)}, u32[]{:S(2)}) collective-permute-start(bf16[1,512,384]{2,1,0:T(8,128)(2,1)S(1)} %add_convert_fusion.3), channel_id=1, source_target_pairs={{0,2},{2,4},{4,6},{6,0},{1,3},{3,5},{5,7},{7,1},{8,10},{10,12},{12... | collective-permute-start | bytes 1179656 | tf_op jit(solution)/shard_map/ppermute | solution.py:277
  165.5 15.9 %collective-permute-start.7 = (bf16[2,512,384]{2,1,0:T(8,128)(2,1)}, bf16[2,512,384]{2,1,0:T(8,128)(2,1)S(1)}, u32[]{:S(2)}, u32[]{:S(2)}) collective-permute-start(bf16[2,512,384]{2,1,0:T(8,128)(2,1)} %get-tuple-element.20), channel_id=1, source_target_pairs={{0,6},{2,0},{4,2},{6,4},{1,7},{3,1},{5,3},{7,5},{8,14},{10,8},{12,... | collective-permute-start | bytes 2359304 | tf_op jit(solution)/shard_map/ppermute | solution.py:277
  165.6 17.4 %collective-permute-start.8 = (bf16[2,512,384]{2,1,0:T(8,128)(2,1)}, bf16[2,512,384]{2,1,0:T(8,128)(2,1)S(1)}, u32[]{:S(2)}, u32[]{:S(2)}) collective-permute-start(bf16[2,512,384]{2,1,0:T(8,128)(2,1)} %get-tuple-element.22), channel_id=1, source_target_pairs={{0,2},{2,4},{4,6},{6,0},{1,3},{3,5},{5,7},{7,1},{8,10},{10,12},{12... | collective-permute-start | bytes 2359304 | tf_op jit(solution)/shard_map/ppermute | solution.py:277
  168.9 30.1 %all-to-all-start.3 = ((bf16[64,16,384]{2,1,0:T(8,128)(2,1)}), bf16[64,16,384]{2,1,0:T(8,128)(2,1)S(1)}, u32[]{:S(2)}, u32[]{:S(2)}) async-start(bf16[64,16,384]{2,1,0:T(8,128)(2,1)} %bitcast.18), calls=%async_computation.3 | async-start | bytes 1572864 | tf_op jit(solution)/shard_map/all_to_all | solution.py:301
  182.4 7.9 %collective-permute-start.10 = (bf16[1,512,384]{2,1,0:T(8,128)(2,1)S(1)}, bf16[1,512,384]{2,1,0:T(8,128)(2,1)S(1)}, u32[]{:S(2)}, u32[]{:S(2)}) collective-permute-start(bf16[1,512,384]{2,1,0:T(8,128)(2,1)S(1)} %add_convert_fusion.5), channel_id=1, source_target_pairs={{0,6},{2,0},{4,2},{6,4},{1,7},{3,1},{5,3},{7,5},{8,14},{10,8},{12,... | collective-permute-start | bytes 1179656 | tf_op jit(solution)/shard_map/ppermute | solution.py:277
  183.1 9.1 %collective-permute-start.9 = (bf16[1,512,384]{2,1,0:T(8,128)(2,1)S(1)}, bf16[1,512,384]{2,1,0:T(8,128)(2,1)S(1)}, u32[]{:S(2)}, u32[]{:S(2)}) collective-permute-start(bf16[1,512,384]{2,1,0:T(8,128)(2,1)S(1)} %add_convert_fusion.7), channel_id=1, source_target_pairs={{0,2},{2,4},{4,6},{6,0},{1,3},{3,5},{5,7},{7,1},{8,10},{10,12},{12... | collective-permute-start | bytes 1179656 | tf_op jit(solution)/shard_map/ppermute | solution.py:277
  199.0 29.5 %all-to-all-start.1 = ((bf16[64,16,384]{2,1,0:T(8,128)(2,1)}), bf16[64,16,384]{2,1,0:T(8,128)(2,1)S(1)}, u32[]{:S(2)}, u32[]{:S(2)}) async-start(bf16[64,16,384]{2,1,0:T(8,128)(2,1)} %bitcast.13), calls=%async_computation.1 | async-start | bytes 1572864 | tf_op jit(solution)/shard_map/all_to_all | solution.py:301
  (16 other events, 162.6 us)
where the time goes:
time: 234 us; the launch traced here: 232 us
  waiting for transfers between devices  101 us (43%)
  Pallas kernels  66.5 us (28%)
  starting transfers between devices  49 us (21%)
  local copies, waits for them, and re-layouts  9.86 us (4%)
  other arithmetic  5.96 us (3%)
    all_to_all x4, waiting for transfers between devices, exchange(): return lax.all_to_all(array, ('c', 'x', 'z'), 0, 0, tiled=True)  59.4 us
    ppermute x16, waiting for transfers between devices, shift(): return lax.ppermute(array, 'y', [(i, (i + by) % RING) for i in range(RING)])  41.4 us
    pallas_call x4, Pallas kernels, kernel(): pl.pallas_call(body, in_specs=[pl.BlockSpec(memory_space=pltpu.MemorySpac...  33.9 us
    all_to_all x4, starting transfers between devices, exchange(): return lax.all_to_all(array, ('c', 'x', 'z'), 0, 0, tiled=True)  26.1 us
    ppermute x16, starting transfers between devices, shift(): return lax.ppermute(array, 'y', [(i, (i + by) % RING) for i in range(RING)])  22.2 us
    pallas_call x3, Pallas kernels, arrange(): pl.pallas_call(body, grid_spec=pltpu.PrefetchScalarGridSpec(num_scalar_pr...  16.8 us
    squeeze x3, local copies, waits for them, and re-layouts, local(): other = lax.dynamic_index_in_dim(w, 1 - core, 0, keepdims=False)  6.38 us
    pallas_call x2, Pallas kernels, combine(): pl.pallas_call(body, out_shape=jax.ShapeDtypeStruct((feats, toks), bf16)...  5.91 us
  transfers between devices with their start and end apart: 23, of which 10 were waited for; matrix products, arithmetic and copies ran while one was open for 5% of the time, Pallas kernels for 26%

commit v1 on v0

--- a/solution.py
+++ b/solution.py
@@ -12,6 +12,7 @@
 RING = 4
 LANES = 384
 HALF = 368
+STEP = 112
 GROUP = 32
 WIDE = CORES * LANES
 VMEM = 56 * 1024 * 1024
@@ -69,7 +70,7 @@
 def factors(ids_t, cw_t, experts, start, size):
     toks = ids_t.shape[1]
 
-    def body(ids_ref, cw_ref, high_ref, low_ref, rank_ref, weight_ref):
+    def body(ids_ref, cw_ref, out_ref, rank_ref, weight_ref):
         hit, rank_ref[...] = slots_of(ids_ref[...], experts)
         cw = cw_ref[...]
         weight_ref[...] = sum(jnp.where(h, cw[k : k + 1, :], 0.0) for k, h in enumerate(hit))
@@ -81,12 +82,12 @@
             coef = jnp.where(spread(rank_ref[some, :], start, size), wide, 0.0).reshape(GROUP * size, toks).T
             high = coef.astype(bf16)
             at = pl.ds(pl.multiple_of(i * GROUP * size, GROUP * size), GROUP * size)
-            high_ref[:, at] = high
-            low_ref[:, at] = (coef - high.astype(f32)).astype(bf16)
-
-    return pl.pallas_call(
-        body,
-        out_shape=[jax.ShapeDtypeStruct((toks, experts * size), bf16)] * 2,
+            out_ref[0, :, at] = high
+            out_ref[1, :, at] = (coef - high.astype(f32)).astype(bf16)
+
+    return pl.pallas_call(
+        body,
+        out_shape=jax.ShapeDtypeStruct((2, toks, experts * size), bf16),
         scratch_shapes=[pltpu.VMEM((experts, toks), f32)] * 2,
         compiler_params=pltpu.CompilerParams(vmem_limit_bytes=VMEM),
         cost_estimate=lasting(4),
@@ -94,24 +95,27 @@
 
 
 def combine(rows, parts, acc, feats):
-    toks = parts[0].shape[0]
+    toks = parts.shape[1]
     last = feats is not None
 
-    def body(rows_ref, high_ref, low_ref, *refs):
-        out_ref = refs[-1]
-        total = jnp.dot(high_ref[...], rows_ref[...], preferred_element_type=f32)
-        total += jnp.dot(low_ref[...], rows_ref[...], preferred_element_type=f32)
-        if acc is not None:
-            total += refs[0][...]
-        out_ref[...] = total.T[:feats, :].astype(bf16) if last else total
+    def body(rows_ref, parts_ref, *refs):
+        out_ref, sum_ref = refs[-2:]
+        sum_ref[...] = jnp.zeros(sum_ref.shape, f32) if acc is None else refs[0][...]
+
+        @pl.loop(0, 2)
+        def _(p):
+            sum_ref[...] += jnp.dot(parts_ref[p], rows_ref[...], preferred_element_type=f32)
+
+        out_ref[...] = sum_ref[...].T[:feats, :].astype(bf16) if last else sum_ref[...]
 
     return pl.pallas_call(
         body,
         out_shape=jax.ShapeDtypeStruct((feats, toks), bf16) if last else jax.ShapeDtypeStruct((toks, LANES), f32),
+        scratch_shapes=[pltpu.VMEM((toks, LANES), f32)],
         compiler_params=pltpu.CompilerParams(vmem_limit_bytes=VMEM),
         cost_estimate=lasting(2),
         name="combine",
-    )(rows, *parts, *(() if acc is None else (acc,)))
+    )(rows, parts, *(() if acc is None else (acc,)))
 
 
 def arrange(core, own, received):
@@ -127,11 +131,19 @@
 
             @pl.when(pl.program_id(0) == q)
             def _(q=q):
-                for c in range(CORES):
-                    j = (CORES * q + c) * feats
-                    to = slice(c * LANES, c * LANES + feats)
-                    out_ref[0, :units, to] = own_ref[0, :, j : j + feats]
-                    out_ref[0, HALF : HALF + units, to] = recv_ref[:, j : j + feats]
+                def move(at, size):
+                    for c in range(CORES):
+                        j = (CORES * q + c) * feats
+                        to = slice(c * LANES, c * LANES + feats)
+                        out_ref[0, pl.ds(at, size), to] = own_ref[0, pl.ds(at, size), j : j + feats]
+                        out_ref[0, pl.ds(HALF + at, size), to] = recv_ref[pl.ds(at, size), j : j + feats]
+
+                @pl.loop(0, units // STEP)
+                def _(i):
+                    move(pl.multiple_of(i * STEP, STEP), STEP)
+
+                if units % STEP:
+                    move(units - units % STEP, units % STEP)
 
     return pl.pallas_call(
         body,
@@ -151,8 +163,9 @@
     )(core, own, received)
 
 
-CAME = [((0, 0), (0, 1)), ((1, 0), (1, 1)), ((3, 0), (3, 1)), ((2, 0),), ((2, 1),)]
-GOES = [((0, 0), (0, 1)), ((2, 0), (1, 1)), ((2, 1), (3, 0)), ((1, 0),), ((3, 1),)]
+CAME = [((0, 0), (0, 1)), ((3, 0),), ((1, 1),), ((3, 1),), ((1, 0),), ((2, 0),), ((2, 1),)]
+GOES = [((0, 0), (0, 1)), ((2, 0),), ((2, 1),), ((1, 1),), ((3, 0),), ((1, 0),), ((3, 1),)]
+MANY = len(CAME)
 
 
 def copies(row, arrays, keys, buf, sem, out, only=None):
@@ -183,48 +196,51 @@
     units = gate_w.shape[1]
 
     def body(row_ref, *refs):
-        xs, ws, out_ref = refs[:5], refs[5:7], refs[7]
-        x, g, u, gate, up, xsem, wsem = refs[8:]
+        xs, ws, out_ref = refs[:MANY], refs[MANY : MANY + 2], refs[MANY + 2]
+        x, gu, acc, xsem, wsem = refs[MANY + 3 :]
         row = row_ref[0]
 
         def load(w, k):
             j = lax.rem(row + k, RING)
-            return pltpu.make_async_copy(ws[w].at[j], (g, u)[w].at[j], wsem.at[w, k])
+            return pltpu.make_async_copy(ws[w].at[j], gu.at[w, j], wsem.at[w, k])
 
         for k in range(RING):
             for cp in copies(row, xs, CAME, x, xsem, False, k):
                 cp.start()
             load(0, k).start()
             load(1, k).start()
-        gate[...] = jnp.zeros(gate.shape, f32)
-        up[...] = jnp.zeros(up.shape, f32)
-
-        @pl.loop(0, RING)
-        def _(k):
+        acc[...] = jnp.zeros(acc.shape, f32)
+
+        @pl.loop(0, 2 * RING)
+        def _(i):
+            k, w = lax.div(i, 2), lax.rem(i, 2)
             j = lax.rem(row + k, RING)
             for some in range(RING):
 
-                @pl.when(k == some)
+                @pl.when(i == 2 * some)
                 def _(some=some):
                     for cp in copies(row, xs, CAME, x, xsem, False, some):
                         cp.wait()
 
-            load(0, k).wait()
-            gate[...] += lax.dot_general(x[j], g[j], NT, preferred_element_type=f32)
-            load(1, k).wait()
-            up[...] += lax.dot_general(x[j], u[j], NT, preferred_element_type=f32)
-
-        a = gate[...]
-        out_ref[...] = ((up[...] + 1.0) * a * jax.nn.sigmoid(1.702 * a)).astype(bf16)
+            for some in range(2):
+
+                @pl.when(w == some)
+                def _(some=some):
+                    load(some, k).wait()
+
+            acc[w] += lax.dot_general(x[j], gu[w, j], NT, preferred_element_type=f32)
+
+        a = acc[0]
+        out_ref[...] = ((acc[1] + 1.0) * a * jax.nn.sigmoid(1.702 * a)).astype(bf16)
 
     return kernel(
         body,
         (row, *pieces, gate_w, up_w),
         jax.ShapeDtypeStruct((h, units), bf16),
         [pltpu.VMEM((RING, h, WIDE), bf16)]
-        + [pltpu.VMEM(gate_w.shape, bf16)] * 2
-        + [pltpu.VMEM((h, units), f32)] * 2
-        + [pltpu.SemaphoreType.DMA((5, 2)), pltpu.SemaphoreType.DMA((2, RING))],
+        + [pltpu.VMEM((2, *gate_w.shape), bf16)]
+        + [pltpu.VMEM((2, h, units), f32)]
+        + [pltpu.SemaphoreType.DMA((MANY, 2)), pltpu.SemaphoreType.DMA((2, RING))],
         9 * h // 512,
     )
 
@@ -233,8 +249,8 @@
     h = hidden.shape[0]
 
     def body(row_ref, hid_ref, w_ref, *refs):
-        outs = refs[:5]
-        hid, d, y, hsem, wsem, ysem = refs[5:]
+        outs = refs[:MANY]
+        hid, d, y, hsem, wsem, ysem = refs[MANY:]
         row = row_ref[0]
         fetch = pltpu.make_async_copy(hid_ref, hid, hsem)
         fetch.start()
@@ -268,7 +284,7 @@
         (row, hidden, down_w),
         [jax.ShapeDtypeStruct((len(k), h, LANES), bf16) for k in GOES],
         [pltpu.VMEM(hidden.shape, bf16), pltpu.VMEM(down_w.shape, bf16), pltpu.VMEM((RING, h, WIDE), bf16)]
-        + [pltpu.SemaphoreType.DMA, pltpu.SemaphoreType.DMA((RING,)), pltpu.SemaphoreType.DMA((5, 2))],
+        + [pltpu.SemaphoreType.DMA, pltpu.SemaphoreType.DMA((RING,)), pltpu.SemaphoreType.DMA((MANY, 2))],
         5 * h // 512,
     )
 
@@ -279,9 +295,11 @@
 
 def gathered(own):
     own = own.reshape(CORES, -1, LANES)
-    back, fore = shift(own, 1), shift(own, -1)
-    far_a, far_b = shift(back[:1], 1), shift(fore[1:], -1)
-    return own, fore, back, far_a, far_b
+    a, b = own[:1], own[1:]
+    back_a, fore_b = shift(a, 1), shift(b, -1)
+    back_b, fore_a = shift(b, 1), shift(a, -1)
+    far_a, far_b = shift(back_a, 1), shift(fore_b, -1)
+    return own, back_a, fore_b, back_b, fore_a, far_a, far_b
 
 
 def added(*parts):
@@ -289,11 +307,11 @@
 
 
 def scattered(parts):
-    own, plus, minus, later_a, later_b = parts
-    plus, minus = shift(plus, 1), shift(minus, -1)
-    back_a = shift(added(later_a, plus[:1]), 1)
-    fore_b = shift(added(later_b, minus[:1]), -1)
-    total = jnp.concatenate([added(own[:1], minus[1:], back_a), added(own[1:], plus[1:], fore_b)])
+    own, far_a, far_b, fore_b, back_a, later_a, later_b = parts
+    far_a, far_b = shift(far_a, 1), shift(far_b, -1)
+    fore_b, back_a = shift(fore_b, 1), shift(back_a, -1)
+    later_a, later_b = shift(added(later_a, far_a), 1), shift(added(later_b, far_b), -1)
+    total = jnp.concatenate([added(own[:1], back_a, later_a), added(own[1:], fore_b, later_b)])
     return total.reshape(-1, LANES)
 
 

time: 234 us -> 242 us (1.034)
  starting transfers between devices: 49 us -> 63.8 us
  waiting for transfers between devices: 101 us -> 94 us
    ppermute x16 -> x24, starting transfers between devices: 22.2 us -> 31.9 us  [shift(): return lax.ppermute(array, 'y', [(i, (i + by) % RING) for i in range(RING)])]
    all_to_all x4, waiting for transfers between devices: 59.4 us -> 51.8 us  [exchange(): return lax.all_to_all(array, ('c', 'x', 'z'), 0, 0, tiled=True)]
    all_to_all x4, starting transfers between devices: 26.1 us -> 31.1 us  [exchange(): return lax.all_to_all(array, ('c', 'x', 'z'), 0, 0, tiled=True)]
    pallas_call x4, Pallas kernels: 33.9 us -> 31.1 us  [kernel(): pl.pallas_call(body, in_specs=[pl.BlockSpec(memory_space=pltpu.MemorySpac...]
    ppermute x16 -> x24, waiting for transfers between devices: 41.4 us -> 42.2 us  [shift(): return lax.ppermute(array, 'y', [(i, (i + by) % RING) for i in range(RING)])]
  transfers between devices with their start and end apart: 23 -> 31, of which waited for: 10 -> 9; matrix products, arithmetic and copies ran while one was open for 5% -> 5% of each run, Pallas kernels for 26% -> 25%
where the time goes in v1:
time: 242 us; the launch traced here: 240 us
  waiting for transfers between devices  94 us (39%)
  Pallas kernels  66.2 us (27%)
  starting transfers between devices  63.8 us (26%)
  local copies, waits for them, and re-layouts  10.7 us (4%)
  other arithmetic  4.98 us (2%)
    all_to_all x4, waiting for transfers between devices, exchange(): return lax.all_to_all(array, ('c', 'x', 'z'), 0, 0, tiled=True)  51.8 us
    ppermute x24, waiting for transfers between devices, shift(): return lax.ppermute(array, 'y', [(i, (i + by) % RING) for i in range(RING)])  42.2 us
    ppermute x24, starting transfers between devices, shift(): return lax.ppermute(array, 'y', [(i, (i + by) % RING) for i in range(RING)])  31.9 us
    pallas_call x4, Pallas kernels, kernel(): pl.pallas_call(body, in_specs=[pl.BlockSpec(memory_space=pltpu.MemorySpac...  31.1 us
    all_to_all x4, starting transfers between devices, exchange(): return lax.all_to_all(array, ('c', 'x', 'z'), 0, 0, tiled=True)  31.1 us
    pallas_call x3, Pallas kernels, arrange(): pl.pallas_call(body, grid_spec=pltpu.PrefetchScalarGridSpec(num_scalar_pr...  18.7 us
    squeeze x3, local copies, waits for them, and re-layouts, local(): other = lax.dynamic_index_in_dim(w, 1 - core, 0, keepdims=False)  7.92 us
    pallas_call x2, Pallas kernels, combine(): pl.pallas_call(body, out_shape=jax.ShapeDtypeStruct((feats, toks), bf16)...  6.38 us
  transfers between devices with their start and end apart: 31, of which 9 were waited for; matrix products, arithmetic and copies ran while one was open for 5% of the time, Pallas kernels for 25%

profile of v1, /device:TPU:32, one launch (start us, length us, event | category | flops | bytes accessed | tf_op | source)
XLA Modules:
  0.0 240.1 jit_solution(12212913480149605056)
XLA Ops:
  2.7 11.6 %all-to-all-start.2 = ((bf16[64,16,384]{2,1,0:T(8,128)(2,1)}), bf16[64,16,384]{2,1,0:T(8,128)(2,1)S(1)}, u32[]{:S(2)}, u32[]{:S(2)}) async-start(bf16[64,16,384]{2,1,0:T(8,128)(2,1)} %bitcast.37), calls=%async_computation.2 | async-start | bytes 1572864 | tf_op jit(solution)/shard_map/all_to_all | solution.py:319
  14.3 3.3 %dynamic-slice_bitcast_fusion.2 = bf16[360,2880]{1,0:T(8,128)(2,1)} fusion(bf16[2,2880,360]{1,2,0:T(8,128)(2,1)} %param.9, s32[]{:T(128)S(6)} %select_n.6), kind=kLoop, calls=%fused_computation.2 | loop fusion | bytes 4147204 | tf_op jit(solution)/shard_map/jit(dynamic_index_in_dim)/squeeze | solution.py:331
  22.3 16.8 %all-to-all-done.2 = bf16[64,16,384]{2,1,0:T(8,128)(2,1)S(1)} async-done(((bf16[64,16,384]{2,1,0:T(8,128)(2,1)}), bf16[64,16,384]{2,1,0:T(8,128)(2,1)S(1)}, u32[]{:S(2)}, u32[]{:S(2)}) %all-to-all-start.2) | async-done | bytes 786464 | tf_op jit(solution)/shard_map/all_to_all | solution.py:319
  39.1 4.6 %all-to-all-start = ((bf16[64,16,384]{2,1,0:T(8,128)(2,1)}), bf16[64,16,384]{2,1,0:T(8,128)(2,1)S(1)}, u32[]{:S(2)}, u32[]{:S(2)}) async-start(bf16[64,16,384]{2,1,0:T(8,128)(2,1)} %bitcast.36), calls=%async_computation | async-start | bytes 1572864 | tf_op jit(solution)/shard_map/all_to_all | solution.py:319
  50.5 18.0 %all-to-all-done = bf16[64,16,384]{2,1,0:T(8,128)(2,1)S(1)} async-done(((bf16[64,16,384]{2,1,0:T(8,128)(2,1)}), bf16[64,16,384]{2,1,0:T(8,128)(2,1)S(1)}, u32[]{:S(2)}, u32[]{:S(2)}) %all-to-all-start) | async-done | bytes 786464 | tf_op jit(solution)/shard_map/all_to_all | solution.py:319
  75.2 6.2 %arrange.5.w_ref = bf16[4,736,768]{2,1,0:T(8,128)(2,1)} custom-call(s32[1]{0:T(128)} %bitcast.7.core_ref, bf16[2,360,2880]{2,1,0:T(8,128)(2,1)} %own_ref.1, bf16[360,2880]{1,0:T(8,128)(2,1)} %collective-permute-done.8.recv_ref), custom_call_target="tpu_custom_call" | custom-call | flops 1500000000 | tf_op jit(solution)/shard_map/arrange/pallas_call | solution.py:148
  81.4 6.3 %arrange.3.refs_7_ = bf16[4,736,768]{2,1,0:T(8,128)(2,1)} custom-call(s32[1]{0:T(128)} %bitcast.7.core_ref, bf16[2,360,2880]{2,1,0:T(8,128)(2,1)} %bitcast.30, bf16[360,2880]{1,0:T(8,128)(2,1)} %collective-permute-done.6.recv_ref), custom_call_target="tpu_custom_call" | custom-call | flops 1500000000 | tf_op jit(solution)/shard_map/arrange/pallas_call | solution.py:148
  87.7 6.2 %arrange.4.refs_8_ = bf16[4,736,768]{2,1,0:T(8,128)(2,1)} custom-call(s32[1]{0:T(128)} %bitcast.7.core_ref, bf16[2,360,2880]{2,1,0:T(8,128)(2,1)} %bitcast.31, bf16[360,2880]{1,0:T(8,128)(2,1)} %collective-permute-done.7.recv_ref), custom_call_target="tpu_custom_call" | custom-call | flops 1500000000 | tf_op jit(solution)/shard_map/arrange/pallas_call | solution.py:148
  98.1 9.5 %shard_map.69.hid_ref = bf16[512,736]{1,0:T(8,128)(2,1)} custom-call(s32[1]{0:T(128)} %bitcast.row_ref, bf16[2,512,384]{2,1,0:T(8,128)(2,1)} %bitcast.33, bf16[1,512,384]{2,1,0:T(8,128)(2,1)} %copy-done.9, bf16[1,512,384]{2,1,0:T(8,128)(2,1)} %copy-done.10, bf16[1,512,384]{2,1,0:T(8,128)(2,1)} %copy-done.13, bf16[1,512,384]{2,1,0:T(8,128)(2,1)} %copy-done.15, ...), custom_call_target="tpu_custom_call" | custom-call | flops 2249999872 | tf_op jit(solution)/shard_map/pallas_call | solution.py:183
  107.6 6.0 %shard_map.70 = (bf16[2,512,384]{2,1,0:T(8,128)(2,1)}, bf16[1,512,384]{2,1,0:T(8,128)(2,1)}, bf16[1,512,384]{2,1,0:T(8,128)(2,1)}, bf16[1,512,384]{2,1,0:T(8,128...) custom-call(s32[1]{0:T(128)} %bitcast.row_ref, ...), custom_call_target="tpu_custom_call" | custom-call | flops 1250000000 | tf_op jit(solution)/shard_map/pallas_call | solution.py:183
  115.8 3.2 %collective-permute-start.3 = (bf16[1,512,384]{2,1,0:T(8,128)(2,1)S(1)}, bf16[1,512,384]{2,1,0:T(8,128)(2,1)S(1)}, u32[]{:S(2)}, u32[]{:S(2)}) collective-permute-start(bf16[1,512,384]{2,1,0:T(8,128)(2,1)S(1)} %bitcast.39), channel_id=1, source_target_pairs={{0,6},{2,0},{4,2},{6,4},{1,7},{3,1},{5,3},{7,5},{8,14},{10,8},{12,... | collective-permute-start | bytes 1179656 | tf_op jit(solution)/shard_map/ppermute | solution.py:293
  119.0 6.9 %collective-permute-done.25 = bf16[1,512,384]{2,1,0:T(8,128)(2,1)S(1)} collective-permute-done((bf16[1,512,384]{2,1,0:T(8,128)(2,1)}, bf16[1,512,384]{2,1,0:T(8,128)(2,1)S(1)}, u32[]{:S(2)}, u32[]{:S(2)}) %collective-permute-start.25) | collective-permute-done | bytes 393248 | tf_op jit(solution)/shard_map/ppermute | solution.py:293
  129.6 6.1 %collective-permute-done.2.refs_3_ = bf16[1,512,384]{2,1,0:T(8,128)(2,1)S(1)} collective-permute-done((bf16[1,512,384]{2,1,0:T(8,128)(2,1)S(1)}, bf16[1,512,384]{2,1,0:T(8,128)(2,1)S(1)}, u32[]{:S(2)}, u32[]{:S(2)}) %collective-permute-start.2) | collective-permute-done | bytes 393248 | tf_op jit(solution)/shard_map/ppermute | solution.py:293
  139.0 5.2 %collective-permute-done.4.refs_5_ = bf16[1,512,384]{2,1,0:T(8,128)(2,1)S(1)} collective-permute-done((bf16[1,512,384]{2,1,0:T(8,128)(2,1)S(1)}, bf16[1,512,384]{2,1,0:T(8,128)(2,1)S(1)}, u32[]{:S(2)}, u32[]{:S(2)}) %collective-permute-start.4) | collective-permute-done | bytes 393248 | tf_op jit(solution)/shard_map/ppermute | solution.py:293
  145.6 9.5 %shard_map.65.hid_ref = bf16[512,736]{1,0:T(8,128)(2,1)} custom-call(s32[1]{0:T(128)} %bitcast.row_ref, bf16[2,512,384]{2,1,0:T(8,128)(2,1)} %bitcast.32, bf16[1,512,384]{2,1,0:T(8,128)(2,1)} %copy-done.7, bf16[1,512,384]{2,1,0:T(8,128)(2,1)} %copy-done.8, bf16[1,512,384]{2,1,0:T(8,128)(2,1)} %copy-done.11, bf16[1,512,384]{2,1,0:T(8,128)(2,1)} %copy-done.12, ...), custom_call_target="tpu_custom_call" | custom-call | flops 2249999872 | tf_op jit(solution)/shard_map/pallas_call | solution.py:183
  155.1 6.1 %shard_map.66 = (bf16[2,512,384]{2,1,0:T(8,128)(2,1)}, bf16[1,512,384]{2,1,0:T(8,128)(2,1)}, bf16[1,512,384]{2,1,0:T(8,128)(2,1)}, bf16[1,512,384]{2,1,0:T(8,128...) custom-call(s32[1]{0:T(128)} %bitcast.row_ref, ...), custom_call_target="tpu_custom_call" | custom-call | flops 1250000000 | tf_op jit(solution)/shard_map/pallas_call | solution.py:183
  165.3 4.6 %all-to-all-start.3 = ((bf16[64,16,384]{2,1,0:T(8,128)(2,1)}), bf16[64,16,384]{2,1,0:T(8,128)(2,1)S(1)}, u32[]{:S(2)}, u32[]{:S(2)}) async-start(bf16[64,16,384]{2,1,0:T(8,128)(2,1)} %bitcast.22), calls=%async_computation.3 | async-start | bytes 1572864 | tf_op jit(solution)/shard_map/all_to_all | solution.py:319
  170.1 3.2 %collective-permute-start.9 = (bf16[1,512,384]{2,1,0:T(8,128)(2,1)S(1)}, bf16[1,512,384]{2,1,0:T(8,128)(2,1)S(1)}, u32[]{:S(2)}, u32[]{:S(2)}) collective-permute-start(bf16[1,512,384]{2,1,0:T(8,128)(2,1)S(1)} %copy-done.21), channel_id=1, source_target_pairs={{0,6},{2,0},{4,2},{6,4},{1,7},{3,1},{5,3},{7,5},{8,14},{10,8},{12,... | collective-permute-start | bytes 1179656 | tf_op jit(solution)/shard_map/ppermute | solution.py:293
  175.4 8.0 %collective-permute-done.10 = bf16[1,512,384]{2,1,0:T(8,128)(2,1)S(1)} collective-permute-done((bf16[1,512,384]{2,1,0:T(8,128)(2,1)}, bf16[1,512,384]{2,1,0:T(8,128)(2,1)S(1)}, u32[]{:S(2)}, u32[]{:S(2)}) %collective-permute-start.10) | collective-permute-done | bytes 393248 | tf_op jit(solution)/shard_map/ppermute | solution.py:293
  183.6 8.2 %collective-permute-done.12 = bf16[1,512,384]{2,1,0:T(8,128)(2,1)S(1)} collective-permute-done((bf16[1,512,384]{2,1,0:T(8,128)(2,1)S(1)}, bf16[1,512,384]{2,1,0:T(8,128)(2,1)S(1)}, u32[]{:S(2)}, u32[]{:S(2)}) %collective-permute-start.12) | collective-permute-done | bytes 393248 | tf_op jit(solution)/shard_map/ppermute | solution.py:293
  191.8 7.8 %collective-permute-done.11 = bf16[1,512,384]{2,1,0:T(8,128)(2,1)S(1)} collective-permute-done((bf16[1,512,384]{2,1,0:T(8,128)(2,1)S(1)}, bf16[1,512,384]{2,1,0:T(8,128)(2,1)S(1)}, u32[]{:S(2)}, u32[]{:S(2)}) %collective-permute-start.11) | collective-permute-done | bytes 393248 | tf_op jit(solution)/shard_map/ppermute | solution.py:293
  200.9 10.3 %all-to-all-start.1 = ((bf16[64,16,384]{2,1,0:T(8,128)(2,1)}), bf16[64,16,384]{2,1,0:T(8,128)(2,1)S(1)}, u32[]{:S(2)}, u32[]{:S(2)}) async-start(bf16[64,16,384]{2,1,0:T(8,128)(2,1)} %bitcast.15), calls=%async_computation.1 | async-start | bytes 1572864 | tf_op jit(solution)/shard_map/all_to_all | solution.py:319
  219.0 17.0 %all-to-all-done.1 = bf16[64,16,384]{2,1,0:T(8,128)(2,1)S(1)} async-done(((bf16[64,16,384]{2,1,0:T(8,128)(2,1)}), bf16[64,16,384]{2,1,0:T(8,128)(2,1)S(1)}, u32[]{:S(2)}, u32[]{:S(2)}) %all-to-all-start.1) | async-done | bytes 786464 | tf_op jit(solution)/shard_map/all_to_all | solution.py:319
  236.9 3.2 %combine.3 = bf16[360,256]{1,0:T(8,128)(2,1)} custom-call(bf16[1024,384]{1,0:T(8,128)(2,1)} %bitcast.35, bf16[2,256,1024]{2,1,0:T(8,128)(2,1)} %shard_map.67.parts_ref, f32[256,384]{1,0:T(8,128)} %combine.2.refs_0_), custom_call_target="tpu_custom_call" | custom-call | flops 500000000 | tf_op jit(solution)/shard_map/combine/pallas_call | solution.py:111
  (110 shorter events, 52.0 us)
Async XLA Ops:
  2.7 36.4 %all-to-all-start.2 = ((bf16[64,16,384]{2,1,0:T(8,128)(2,1)}), bf16[64,16,384]{2,1,0:T(8,128)(2,1)S(1)}, u32[]{:S(2)}, u32[]{:S(2)}) async-start(bf16[64,16,384]{2,1,0:T(8,128)(2,1)} %bitcast.37), calls=%async_computation.2 | async-start | bytes 1572864 | tf_op jit(solution)/shard_map/all_to_all | solution.py:319
  17.6 54.4 %collective-permute-start.6 = (bf16[360,2880]{1,0:T(8,128)(2,1)}, bf16[360,2880]{1,0:T(8,128)(2,1)}, u32[]{:S(2)}, u32[]{:S(2)}) collective-permute-start(bf16[360,2880]{1,0:T(8,128)(2,1)} %dynamic-slice_bitcast_fusion.2), channel_id=1, source_target_pairs={{0,1},{1,0},{2,3},{3,2},{4,5},{5,4},{6,7},{7,6},{8,9},{9,8},{10,11... | collective-permute-start | bytes 6220808 | tf_op jit(solution)/shard_map/ppermute | solution.py:332
  19.3 53.0 %collective-permute-start.8 = (bf16[360,2880]{1,0:T(8,128)(2,1)}, bf16[360,2880]{1,0:T(8,128)(2,1)}, u32[]{:S(2)}, u32[]{:S(2)}) collective-permute-start(bf16[360,2880]{1,0:T(8,128)(2,1)} %dynamic-slice_bitcast_fusion), channel_id=1, source_target_pairs={{0,1},{1,0},{2,3},{3,2},{4,5},{5,4},{6,7},{7,6},{8,9},{9,8},{10,11... | collective-permute-start | bytes 6220808 | tf_op jit(solution)/shard_map/ppermute | solution.py:332
  39.1 29.5 %all-to-all-start = ((bf16[64,16,384]{2,1,0:T(8,128)(2,1)}), bf16[64,16,384]{2,1,0:T(8,128)(2,1)S(1)}, u32[]{:S(2)}, u32[]{:S(2)}) async-start(bf16[64,16,384]{2,1,0:T(8,128)(2,1)} %bitcast.36), calls=%async_computation | async-start | bytes 1572864 | tf_op jit(solution)/shard_map/all_to_all | solution.py:319
  46.8 40.9 %collective-permute-start.7 = (bf16[360,2880]{1,0:T(8,128)(2,1)}, bf16[360,2880]{1,0:T(8,128)(2,1)}, u32[]{:S(2)}, u32[]{:S(2)}) collective-permute-start(bf16[360,2880]{1,0:T(8,128)(2,1)} %dynamic-slice_bitcast_fusion.1), channel_id=1, source_target_pairs={{0,1},{1,0},{2,3},{3,2},{4,5},{5,4},{6,7},{7,6},{8,9},{9,8},{10,11... | collective-permute-start | bytes 6220808 | tf_op jit(solution)/shard_map/ppermute | solution.py:332
  47.2 21.5 %collective-permute-start.15 = (bf16[1,512,384]{2,1,0:T(8,128)(2,1)S(1)}, bf16[1,512,384]{2,1,0:T(8,128)(2,1)S(1)}, u32[]{:S(2)}, u32[]{:S(2)}) collective-permute-start(bf16[1,512,384]{2,1,0:T(8,128)(2,1)S(1)} %bitcast.42), channel_id=1, source_target_pairs={{0,2},{2,4},{4,6},{6,0},{1,3},{3,5},{5,7},{7,1},{8,10},{10,12},{12... | collective-permute-start | bytes 1179656 | tf_op jit(solution)/shard_map/ppermute | solution.py:293
  48.8 21.5 %collective-permute-start.16 = (bf16[1,512,384]{2,1,0:T(8,128)(2,1)S(1)}, bf16[1,512,384]{2,1,0:T(8,128)(2,1)S(1)}, u32[]{:S(2)}, u32[]{:S(2)}) collective-permute-start(bf16[1,512,384]{2,1,0:T(8,128)(2,1)S(1)} %bitcast.44), channel_id=1, source_target_pairs={{0,6},{2,0},{4,2},{6,4},{1,7},{3,1},{5,3},{7,5},{8,14},{10,8},{12,... | collective-permute-start | bytes 1179656 | tf_op jit(solution)/shard_map/ppermute | solution.py:293
  68.7 25.3 %collective-permute-start.17 = (bf16[1,512,384]{2,1,0:T(8,128)(2,1)S(1)}, bf16[1,512,384]{2,1,0:T(8,128)(2,1)S(1)}, u32[]{:S(2)}, u32[]{:S(2)}) collective-permute-start(bf16[1,512,384]{2,1,0:T(8,128)(2,1)S(1)} %bitcast.45), channel_id=1, source_target_pairs={{0,2},{2,4},{4,6},{6,0},{1,3},{3,5},{5,7},{7,1},{8,10},{10,12},{12... | collective-permute-start | bytes 1179656 | tf_op jit(solution)/shard_map/ppermute | solution.py:293
  70.3 26.8 %collective-permute-start.18 = (bf16[1,512,384]{2,1,0:T(8,128)(2,1)S(1)}, bf16[1,512,384]{2,1,0:T(8,128)(2,1)S(1)}, u32[]{:S(2)}, u32[]{:S(2)}) collective-permute-start(bf16[1,512,384]{2,1,0:T(8,128)(2,1)S(1)} %bitcast.43), channel_id=1, source_target_pairs={{0,6},{2,0},{4,2},{6,4},{1,7},{3,1},{5,3},{7,5},{8,14},{10,8},{12,... | collective-permute-start | bytes 1179656 | tf_op jit(solution)/shard_map/ppermute | solution.py:293
  72.0 25.1 %collective-permute-start.19 = (bf16[1,512,384]{2,1,0:T(8,128)(2,1)S(1)}, bf16[1,512,384]{2,1,0:T(8,128)(2,1)S(1)}, u32[]{:S(2)}, u32[]{:S(2)}) collective-permute-start(bf16[1,512,384]{2,1,0:T(8,128)(2,1)S(1)} %collective-permute-done.15.refs_1_), channel_id=1, source_target_pairs={{0,2},{2,4},{4,6},{6,0},{1,3},{3,5},{5,7},{7,1},{8,10},{10,12},{12... | collective-permute-start | bytes 1179656 | tf_op jit(solution)/shard_map/ppermute | solution.py:293
  72.4 24.8 %collective-permute-start.20 = (bf16[1,512,384]{2,1,0:T(8,128)(2,1)S(1)}, bf16[1,512,384]{2,1,0:T(8,128)(2,1)S(1)}, u32[]{:S(2)}, u32[]{:S(2)}) collective-permute-start(bf16[1,512,384]{2,1,0:T(8,128)(2,1)S(1)} %collective-permute-done.16.refs_2_), channel_id=1, source_target_pairs={{0,6},{2,0},{4,2},{6,4},{1,7},{3,1},{5,3},{7,5},{8,14},{10,8},{12,... | collective-permute-start | bytes 1179656 | tf_op jit(solution)/shard_map/ppermute | solution.py:293
  87.7 28.1 %collective-permute-start = (bf16[1,512,384]{2,1,0:T(8,128)(2,1)S(1)}, bf16[1,512,384]{2,1,0:T(8,128)(2,1)S(1)}, u32[]{:S(2)}, u32[]{:S(2)}) collective-permute-start(bf16[1,512,384]{2,1,0:T(8,128)(2,1)S(1)} %bitcast.38), channel_id=1, source_target_pairs={{0,2},{2,4},{4,6},{6,0},{1,3},{3,5},{5,7},{7,1},{8,10},{10,12},{12... | collective-permute-start | bytes 1179656 | tf_op jit(solution)/shard_map/ppermute | solution.py:293
  93.9 25.1 %collective-permute-start.1 = (bf16[1,512,384]{2,1,0:T(8,128)(2,1)S(1)}, bf16[1,512,384]{2,1,0:T(8,128)(2,1)S(1)}, u32[]{:S(2)}, u32[]{:S(2)}) collective-permute-start(bf16[1,512,384]{2,1,0:T(8,128)(2,1)S(1)} %bitcast.40), channel_id=1, source_target_pairs={{0,6},{2,0},{4,2},{6,4},{1,7},{3,1},{5,3},{7,5},{8,14},{10,8},{12,... | collective-permute-start | bytes 1179656 | tf_op jit(solution)/shard_map/ppermute | solution.py:293
  115.8 20.0 %collective-permute-start.2 = (bf16[1,512,384]{2,1,0:T(8,128)(2,1)S(1)}, bf16[1,512,384]{2,1,0:T(8,128)(2,1)S(1)}, u32[]{:S(2)}, u32[]{:S(2)}) collective-permute-start(bf16[1,512,384]{2,1,0:T(8,128)(2,1)S(1)} %bitcast.41), channel_id=1, source_target_pairs={{0,2},{2,4},{4,6},{6,0},{1,3},{3,5},{5,7},{7,1},{8,10},{10,12},{12... | collective-permute-start | bytes 1179656 | tf_op jit(solution)/shard_map/ppermute | solution.py:293
  115.8 20.6 %collective-permute-start.3 = (bf16[1,512,384]{2,1,0:T(8,128)(2,1)S(1)}, bf16[1,512,384]{2,1,0:T(8,128)(2,1)S(1)}, u32[]{:S(2)}, u32[]{:S(2)}) collective-permute-start(bf16[1,512,384]{2,1,0:T(8,128)(2,1)S(1)} %bitcast.39), channel_id=1, source_target_pairs={{0,6},{2,0},{4,2},{6,4},{1,7},{3,1},{5,3},{7,5},{8,14},{10,8},{12,... | collective-permute-start | bytes 1179656 | tf_op jit(solution)/shard_map/ppermute | solution.py:293
  119.0 25.1 %collective-permute-start.4 = (bf16[1,512,384]{2,1,0:T(8,128)(2,1)S(1)}, bf16[1,512,384]{2,1,0:T(8,128)(2,1)S(1)}, u32[]{:S(2)}, u32[]{:S(2)}) collective-permute-start(bf16[1,512,384]{2,1,0:T(8,128)(2,1)S(1)} %collective-permute-done.refs_1_), channel_id=1, source_target_pairs={{0,2},{2,4},{4,6},{6,0},{1,3},{3,5},{5,7},{7,1},{8,10},{10,12},{12... | collective-permute-start | bytes 1179656 | tf_op jit(solution)/shard_map/ppermute | solution.py:293
  128.4 35.5 %collective-permute-start.21 = (bf16[1,512,384]{2,1,0:T(8,128)(2,1)}, bf16[1,512,384]{2,1,0:T(8,128)(2,1)S(1)}, u32[]{:S(2)}, u32[]{:S(2)}) collective-permute-start(bf16[1,512,384]{2,1,0:T(8,128)(2,1)} %get-tuple-element.27), channel_id=1, source_target_pairs={{0,6},{2,0},{4,2},{6,4},{1,7},{3,1},{5,3},{7,5},{8,14},{10,8},{12,... | collective-permute-start | bytes 1179656 | tf_op jit(solution)/shard_map/ppermute | solution.py:293
  135.8 28.2 %collective-permute-start.24 = (bf16[1,512,384]{2,1,0:T(8,128)(2,1)}, bf16[1,512,384]{2,1,0:T(8,128)(2,1)S(1)}, u32[]{:S(2)}, u32[]{:S(2)}) collective-permute-start(bf16[1,512,384]{2,1,0:T(8,128)(2,1)} %get-tuple-element.30), channel_id=1, source_target_pairs={{0,2},{2,4},{4,6},{6,0},{1,3},{3,5},{5,7},{7,1},{8,10},{10,12},{12... | collective-permute-start | bytes 1179656 | tf_op jit(solution)/shard_map/ppermute | solution.py:293
  136.4 27.5 %collective-permute-start.26 = (bf16[1,512,384]{2,1,0:T(8,128)(2,1)S(1)}, bf16[1,512,384]{2,1,0:T(8,128)(2,1)S(1)}, u32[]{:S(2)}, u32[]{:S(2)}) collective-permute-start(bf16[1,512,384]{2,1,0:T(8,128)(2,1)S(1)} %add_convert_fusion.1), channel_id=1, source_target_pairs={{0,6},{2,0},{4,2},{6,4},{1,7},{3,1},{5,3},{7,5},{8,14},{10,8},{12,... | collective-permute-start | bytes 1179656 | tf_op jit(solution)/shard_map/ppermute | solution.py:293
  144.2 19.7 %collective-permute-start.23 = (bf16[1,512,384]{2,1,0:T(8,128)(2,1)S(1)}, bf16[1,512,384]{2,1,0:T(8,128)(2,1)S(1)}, u32[]{:S(2)}, u32[]{:S(2)}) collective-permute-start(bf16[1,512,384]{2,1,0:T(8,128)(2,1)S(1)} %add_convert_fusion.3), channel_id=1, source_target_pairs={{0,2},{2,4},{4,6},{6,0},{1,3},{3,5},{5,7},{7,1},{8,10},{10,12},{12... | collective-permute-start | bytes 1179656 | tf_op jit(solution)/shard_map/ppermute | solution.py:293
  165.3 35.6 %all-to-all-start.3 = ((bf16[64,16,384]{2,1,0:T(8,128)(2,1)}), bf16[64,16,384]{2,1,0:T(8,128)(2,1)S(1)}, u32[]{:S(2)}, u32[]{:S(2)}) async-start(bf16[64,16,384]{2,1,0:T(8,128)(2,1)} %bitcast.22), calls=%async_computation.3 | async-start | bytes 1572864 | tf_op jit(solution)/shard_map/all_to_all | solution.py:319
  170.0 21.8 %collective-permute-start.12 = (bf16[1,512,384]{2,1,0:T(8,128)(2,1)S(1)}, bf16[1,512,384]{2,1,0:T(8,128)(2,1)S(1)}, u32[]{:S(2)}, u32[]{:S(2)}) collective-permute-start(bf16[1,512,384]{2,1,0:T(8,128)(2,1)S(1)} %copy-done.22), channel_id=1, source_target_pairs={{0,2},{2,4},{4,6},{6,0},{1,3},{3,5},{5,7},{7,1},{8,10},{10,12},{12... | collective-permute-start | bytes 1179656 | tf_op jit(solution)/shard_map/ppermute | solution.py:293
  170.1 21.7 %collective-permute-start.9 = (bf16[1,512,384]{2,1,0:T(8,128)(2,1)S(1)}, bf16[1,512,384]{2,1,0:T(8,128)(2,1)S(1)}, u32[]{:S(2)}, u32[]{:S(2)}) collective-permute-start(bf16[1,512,384]{2,1,0:T(8,128)(2,1)S(1)} %copy-done.21), channel_id=1, source_target_pairs={{0,6},{2,0},{4,2},{6,4},{1,7},{3,1},{5,3},{7,5},{8,14},{10,8},{12,... | collective-permute-start | bytes 1179656 | tf_op jit(solution)/shard_map/ppermute | solution.py:293
  200.9 35.1 %all-to-all-start.1 = ((bf16[64,16,384]{2,1,0:T(8,128)(2,1)}), bf16[64,16,384]{2,1,0:T(8,128)(2,1)S(1)}, u32[]{:S(2)}, u32[]{:S(2)}) async-start(bf16[64,16,384]{2,1,0:T(8,128)(2,1)} %bitcast.15), calls=%async_computation.1 | async-start | bytes 1572864 | tf_op jit(solution)/shard_map/all_to_all | solution.py:319
  (30 other events, 367.5 us)

commit v2 on v1

--- a/solution.py
+++ b/solution.py
@@ -80,42 +80,19 @@
             some = pl.ds(pl.multiple_of(i * GROUP, GROUP), GROUP)
             wide = jnp.broadcast_to(weight_ref[some, :][:, None, :], (GROUP, size, toks))
             coef = jnp.where(spread(rank_ref[some, :], start, size), wide, 0.0).reshape(GROUP * size, toks).T
-            high = coef.astype(bf16)
-            at = pl.ds(pl.multiple_of(i * GROUP * size, GROUP * size), GROUP * size)
-            out_ref[0, :, at] = high
-            out_ref[1, :, at] = (coef - high.astype(f32)).astype(bf16)
+            out_ref[:, pl.ds(pl.multiple_of(i * GROUP * size, GROUP * size), GROUP * size)] = coef.astype(bf16)
 
     return pl.pallas_call(
         body,
-        out_shape=jax.ShapeDtypeStruct((2, toks, experts * size), bf16),
+        out_shape=jax.ShapeDtypeStruct((toks, experts * size), bf16),
         scratch_shapes=[pltpu.VMEM((experts, toks), f32)] * 2,
         compiler_params=pltpu.CompilerParams(vmem_limit_bytes=VMEM),
         cost_estimate=lasting(4),
     )(ids_t, cw_t)
 
 
-def combine(rows, parts, acc, feats):
-    toks = parts.shape[1]
-    last = feats is not None
-
-    def body(rows_ref, parts_ref, *refs):
-        out_ref, sum_ref = refs[-2:]
-        sum_ref[...] = jnp.zeros(sum_ref.shape, f32) if acc is None else refs[0][...]
-
-        @pl.loop(0, 2)
-        def _(p):
-            sum_ref[...] += jnp.dot(parts_ref[p], rows_ref[...], preferred_element_type=f32)
-
-        out_ref[...] = sum_ref[...].T[:feats, :].astype(bf16) if last else sum_ref[...]
-
-    return pl.pallas_call(
-        body,
-        out_shape=jax.ShapeDtypeStruct((feats, toks), bf16) if last else jax.ShapeDtypeStruct((toks, LANES), f32),
-        scratch_shapes=[pltpu.VMEM((toks, LANES), f32)],
-        compiler_params=pltpu.CompilerParams(vmem_limit_bytes=VMEM),
-        cost_estimate=lasting(2),
-        name="combine",
-    )(rows, parts, *(() if acc is None else (acc,)))
+def combine(rows, factor):
+    return lax.dot_general(rows, factor, (((0,), (1,)), ((), ())), preferred_element_type=f32)
 
 
 def arrange(core, own, received):
@@ -343,10 +320,10 @@
         part = scattered(part)
         returned.append(exchange(part))
         parts.append(factors(ids_t, cw_t, experts, start, size))
-    acc = None
+    total = 0.0
     for i in range(len(PARTS)):
-        acc = combine(returned[i], parts[i], acc, feats if i == len(PARTS) - 1 else None)
-    return acc.T
+        total += combine(returned[i], parts[i])
+    return total[:feats].astype(bf16).T
 
 
 def solution(mesh):

time: 242 us -> 240 us (level)
  Pallas kernels: 66.2 us -> 59.2 us
  matrix products: 0 us -> 2.9 us
  waiting for transfers between devices: 94 us -> 96.5 us
    pallas_call x4 -> x2, Pallas kernels: 11 us -> 3.97 us  [factors(): pl.pallas_call(body, out_shape=jax.ShapeDtypeStruct((toks, experts * size...]
    dot_general x0 -> x2, matrix products: none -> 2.9 us  [combine(): lax.dot_general(rows, factor, (((0,), (1,)), ((), ())), preferred_element...]
  transfers between devices with their start and end apart: 31 -> 31, of which waited for: 9 -> 9; matrix products, arithmetic and copies ran while one was open for 5% -> 6% of each run, Pallas kernels for 25% -> 24%
where the time goes in v2:
time: 240 us; the launch traced here: 238 us
  waiting for transfers between devices  96.5 us (40%)
  starting transfers between devices  63.7 us (27%)
  Pallas kernels  59.2 us (25%)
  local copies, waits for them, and re-layouts  9.86 us (4%)
  other arithmetic  5.69 us (2%)
  matrix products  2.9 us (1%)
    all_to_all x4, waiting for transfers between devices, exchange(): return lax.all_to_all(array, ('c', 'x', 'z'), 0, 0, tiled=True)  54.2 us
    ppermute x24, waiting for transfers between devices, shift(): return lax.ppermute(array, 'y', [(i, (i + by) % RING) for i in range(RING)])  42.3 us
    ppermute x24, starting transfers between devices, shift(): return lax.ppermute(array, 'y', [(i, (i + by) % RING) for i in range(RING)])  31.8 us
    pallas_call x4, Pallas kernels, kernel(): pl.pallas_call(body, in_specs=[pl.BlockSpec(memory_space=pltpu.MemorySpac...  31.2 us
    all_to_all x4, starting transfers between devices, exchange(): return lax.all_to_all(array, ('c', 'x', 'z'), 0, 0, tiled=True)  31.1 us
    pallas_call x3, Pallas kernels, arrange(): pl.pallas_call(body, grid_spec=pltpu.PrefetchScalarGridSpec(num_scalar_pr...  18.7 us
    squeeze x3, local copies, waits for them, and re-layouts, local(): other = lax.dynamic_index_in_dim(w, 1 - core, 0, keepdims=False)  7.94 us
    pallas_call x2, Pallas kernels, dispatch(): pl.pallas_call(body, out_shape=jax.ShapeDtypeStruct((experts * size, LANE...  5.32 us
  transfers between devices with their start and end apart: 31, of which 9 were waited for; matrix products, arithmetic and copies ran while one was open for 6% of the time, Pallas kernels for 24%

profile of v2, /device:TPU:32, one launch (start us, length us, event | category | flops | bytes accessed | tf_op | source)
XLA Modules:
  0.0 238.3 jit_solution(7346222097431053296)
XLA Ops:
  2.7 11.6 %all-to-all-start = ((bf16[64,16,384]{2,1,0:T(8,128)(2,1)}), bf16[64,16,384]{2,1,0:T(8,128)(2,1)S(1)}, u32[]{:S(2)}, u32[]{:S(2)}) async-start(bf16[64,16,384]{2,1,0:T(8,128)(2,1)} %bitcast.42), calls=%async_computation | async-start | bytes 1572864 | tf_op jit(solution)/shard_map/all_to_all | solution.py:296
  14.3 3.3 %dynamic-slice_bitcast_fusion.2 = bf16[360,2880]{1,0:T(8,128)(2,1)} fusion(bf16[2,2880,360]{1,2,0:T(8,128)(2,1)} %param.9, s32[]{:T(128)S(6)} %select_n.6), kind=kLoop, calls=%fused_computation.2 | loop fusion | bytes 4147204 | tf_op jit(solution)/shard_map/jit(dynamic_index_in_dim)/squeeze | solution.py:308
  22.3 16.8 %all-to-all-done = bf16[64,16,384]{2,1,0:T(8,128)(2,1)S(1)} async-done(((bf16[64,16,384]{2,1,0:T(8,128)(2,1)}), bf16[64,16,384]{2,1,0:T(8,128)(2,1)S(1)}, u32[]{:S(2)}, u32[]{:S(2)}) %all-to-all-start) | async-done | bytes 786464 | tf_op jit(solution)/shard_map/all_to_all | solution.py:296
  39.0 4.6 %all-to-all-start.2 = ((bf16[64,16,384]{2,1,0:T(8,128)(2,1)}), bf16[64,16,384]{2,1,0:T(8,128)(2,1)S(1)}, u32[]{:S(2)}, u32[]{:S(2)}) async-start(bf16[64,16,384]{2,1,0:T(8,128)(2,1)} %bitcast.41), calls=%async_computation.2 | async-start | bytes 1572864 | tf_op jit(solution)/shard_map/all_to_all | solution.py:296
  50.5 18.1 %all-to-all-done.2 = bf16[64,16,384]{2,1,0:T(8,128)(2,1)S(1)} async-done(((bf16[64,16,384]{2,1,0:T(8,128)(2,1)}), bf16[64,16,384]{2,1,0:T(8,128)(2,1)S(1)}, u32[]{:S(2)}, u32[]{:S(2)}) %all-to-all-start.2) | async-done | bytes 786464 | tf_op jit(solution)/shard_map/all_to_all | solution.py:296
  75.2 6.2 %arrange.5.w_ref = bf16[4,736,768]{2,1,0:T(8,128)(2,1)} custom-call(s32[1]{0:T(128)} %bitcast.7.core_ref, bf16[2,360,2880]{2,1,0:T(8,128)(2,1)} %own_ref.1, bf16[360,2880]{1,0:T(8,128)(2,1)} %collective-permute-done.8.recv_ref), custom_call_target="tpu_custom_call" | custom-call | flops 1500000000 | tf_op jit(solution)/shard_map/arrange/pallas_call | solution.py:125
  81.5 6.3 %arrange.3.refs_7_ = bf16[4,736,768]{2,1,0:T(8,128)(2,1)} custom-call(s32[1]{0:T(128)} %bitcast.7.core_ref, bf16[2,360,2880]{2,1,0:T(8,128)(2,1)} %bitcast.35, bf16[360,2880]{1,0:T(8,128)(2,1)} %collective-permute-done.6.recv_ref), custom_call_target="tpu_custom_call" | custom-call | flops 1500000000 | tf_op jit(solution)/shard_map/arrange/pallas_call | solution.py:125
  87.8 6.2 %arrange.4.refs_8_ = bf16[4,736,768]{2,1,0:T(8,128)(2,1)} custom-call(s32[1]{0:T(128)} %bitcast.7.core_ref, bf16[2,360,2880]{2,1,0:T(8,128)(2,1)} %bitcast.36, bf16[360,2880]{1,0:T(8,128)(2,1)} %collective-permute-done.7.recv_ref), custom_call_target="tpu_custom_call" | custom-call | flops 1500000000 | tf_op jit(solution)/shard_map/arrange/pallas_call | solution.py:125
  98.2 9.5 %shard_map.65.hid_ref = bf16[512,736]{1,0:T(8,128)(2,1)} custom-call(s32[1]{0:T(128)} %bitcast.row_ref, bf16[2,512,384]{2,1,0:T(8,128)(2,1)} %bitcast.38, bf16[1,512,384]{2,1,0:T(8,128)(2,1)} %copy-done.7, bf16[1,512,384]{2,1,0:T(8,128)(2,1)} %copy-done.8, bf16[1,512,384]{2,1,0:T(8,128)(2,1)} %copy-done.11, bf16[1,512,384]{2,1,0:T(8,128)(2,1)} %copy-done.13, ...), custom_call_target="tpu_custom_call" | custom-call | flops 2249999872 | tf_op jit(solution)/shard_map/pallas_call | solution.py:160
  107.7 6.1 %shard_map.66 = (bf16[2,512,384]{2,1,0:T(8,128)(2,1)}, bf16[1,512,384]{2,1,0:T(8,128)(2,1)}, bf16[1,512,384]{2,1,0:T(8,128)(2,1)}, bf16[1,512,384]{2,1,0:T(8,128...) custom-call(s32[1]{0:T(128)} %bitcast.row_ref, ...), custom_call_target="tpu_custom_call" | custom-call | flops 1250000000 | tf_op jit(solution)/shard_map/pallas_call | solution.py:160
  115.9 3.2 %collective-permute-start.18 = (bf16[1,512,384]{2,1,0:T(8,128)(2,1)S(1)}, bf16[1,512,384]{2,1,0:T(8,128)(2,1)S(1)}, u32[]{:S(2)}, u32[]{:S(2)}) collective-permute-start(bf16[1,512,384]{2,1,0:T(8,128)(2,1)S(1)} %bitcast.44), channel_id=1, source_target_pairs={{0,6},{2,0},{4,2},{6,4},{1,7},{3,1},{5,3},{7,5},{8,14},{10,8},{12,... | collective-permute-start | bytes 1179656 | tf_op jit(solution)/shard_map/ppermute | solution.py:270
  119.1 6.9 %collective-permute-done.13 = bf16[1,512,384]{2,1,0:T(8,128)(2,1)S(1)} collective-permute-done((bf16[1,512,384]{2,1,0:T(8,128)(2,1)}, bf16[1,512,384]{2,1,0:T(8,128)(2,1)S(1)}, u32[]{:S(2)}, u32[]{:S(2)}) %collective-permute-start.13) | collective-permute-done | bytes 393248 | tf_op jit(solution)/shard_map/ppermute | solution.py:270
  130.4 5.5 %collective-permute-done.17.refs_3_ = bf16[1,512,384]{2,1,0:T(8,128)(2,1)S(1)} collective-permute-done((bf16[1,512,384]{2,1,0:T(8,128)(2,1)S(1)}, bf16[1,512,384]{2,1,0:T(8,128)(2,1)S(1)}, u32[]{:S(2)}, u32[]{:S(2)}) %collective-permute-start.17) | collective-permute-done | bytes 393248 | tf_op jit(solution)/shard_map/ppermute | solution.py:270
  137.1 7.1 %collective-permute-done.19.refs_5_ = bf16[1,512,384]{2,1,0:T(8,128)(2,1)S(1)} collective-permute-done((bf16[1,512,384]{2,1,0:T(8,128)(2,1)S(1)}, bf16[1,512,384]{2,1,0:T(8,128)(2,1)S(1)}, u32[]{:S(2)}, u32[]{:S(2)}) %collective-permute-start.19) | collective-permute-done | bytes 393248 | tf_op jit(solution)/shard_map/ppermute | solution.py:270
  145.7 9.5 %shard_map.69.hid_ref = bf16[512,736]{1,0:T(8,128)(2,1)} custom-call(s32[1]{0:T(128)} %bitcast.row_ref, bf16[2,512,384]{2,1,0:T(8,128)(2,1)} %bitcast.37, bf16[1,512,384]{2,1,0:T(8,128)(2,1)} %copy-done.5, bf16[1,512,384]{2,1,0:T(8,128)(2,1)} %copy-done.6, bf16[1,512,384]{2,1,0:T(8,128)(2,1)} %copy-done.9, bf16[1,512,384]{2,1,0:T(8,128)(2,1)} %copy-done.10, ...), custom_call_target="tpu_custom_call" | custom-call | flops 2249999872 | tf_op jit(solution)/shard_map/pallas_call | solution.py:160
  155.2 6.2 %shard_map.70 = (bf16[2,512,384]{2,1,0:T(8,128)(2,1)}, bf16[1,512,384]{2,1,0:T(8,128)(2,1)}, bf16[1,512,384]{2,1,0:T(8,128)(2,1)}, bf16[1,512,384]{2,1,0:T(8,128...) custom-call(s32[1]{0:T(128)} %bitcast.row_ref, ...), custom_call_target="tpu_custom_call" | custom-call | flops 1250000000 | tf_op jit(solution)/shard_map/pallas_call | solution.py:160
  165.4 4.6 %all-to-all-start.1 = ((bf16[64,16,384]{2,1,0:T(8,128)(2,1)}), bf16[64,16,384]{2,1,0:T(8,128)(2,1)S(1)}, u32[]{:S(2)}, u32[]{:S(2)}) async-start(bf16[64,16,384]{2,1,0:T(8,128)(2,1)} %bitcast.15), calls=%async_computation.1 | async-start | bytes 1572864 | tf_op jit(solution)/shard_map/all_to_all | solution.py:296
  170.1 3.2 %collective-permute-start.21 = (bf16[1,512,384]{2,1,0:T(8,128)(2,1)S(1)}, bf16[1,512,384]{2,1,0:T(8,128)(2,1)S(1)}, u32[]{:S(2)}, u32[]{:S(2)}) collective-permute-start(bf16[1,512,384]{2,1,0:T(8,128)(2,1)S(1)} %copy-done.20), channel_id=1, source_target_pairs={{0,6},{2,0},{4,2},{6,4},{1,7},{3,1},{5,3},{7,5},{8,14},{10,8},{12,... | collective-permute-start | bytes 1179656 | tf_op jit(solution)/shard_map/ppermute | solution.py:270
  173.4 3.3 %collective-permute-start.26 = (bf16[1,512,384]{2,1,0:T(8,128)(2,1)S(1)}, bf16[1,512,384]{2,1,0:T(8,128)(2,1)S(1)}, u32[]{:S(2)}, u32[]{:S(2)}) collective-permute-start(bf16[1,512,384]{2,1,0:T(8,128)(2,1)S(1)} %add_convert_fusion.1), channel_id=1, source_target_pairs={{0,6},{2,0},{4,2},{6,4},{1,7},{3,1},{5,3},{7,5},{8,14},{10,8},{12,... | collective-permute-start | bytes 1179656 | tf_op jit(solution)/shard_map/ppermute | solution.py:270
  176.7 6.7 %collective-permute-done.22 = bf16[1,512,384]{2,1,0:T(8,128)(2,1)S(1)} collective-permute-done((bf16[1,512,384]{2,1,0:T(8,128)(2,1)}, bf16[1,512,384]{2,1,0:T(8,128)(2,1)S(1)}, u32[]{:S(2)}, u32[]{:S(2)}) %collective-permute-start.22) | collective-permute-done | bytes 393248 | tf_op jit(solution)/shard_map/ppermute | solution.py:270
  183.7 8.2 %collective-permute-done.24 = bf16[1,512,384]{2,1,0:T(8,128)(2,1)S(1)} collective-permute-done((bf16[1,512,384]{2,1,0:T(8,128)(2,1)S(1)}, bf16[1,512,384]{2,1,0:T(8,128)(2,1)S(1)}, u32[]{:S(2)}, u32[]{:S(2)}) %collective-permute-start.24) | collective-permute-done | bytes 393248 | tf_op jit(solution)/shard_map/ppermute | solution.py:270
  191.9 7.8 %collective-permute-done.23 = bf16[1,512,384]{2,1,0:T(8,128)(2,1)S(1)} collective-permute-done((bf16[1,512,384]{2,1,0:T(8,128)(2,1)S(1)}, bf16[1,512,384]{2,1,0:T(8,128)(2,1)S(1)}, u32[]{:S(2)}, u32[]{:S(2)}) %collective-permute-start.23) | collective-permute-done | bytes 393248 | tf_op jit(solution)/shard_map/ppermute | solution.py:270
  201.0 10.3 %all-to-all-start.3 = ((bf16[64,16,384]{2,1,0:T(8,128)(2,1)}), bf16[64,16,384]{2,1,0:T(8,128)(2,1)S(1)}, u32[]{:S(2)}, u32[]{:S(2)}) async-start(bf16[64,16,384]{2,1,0:T(8,128)(2,1)} %bitcast.22), calls=%async_computation.3 | async-start | bytes 1572864 | tf_op jit(solution)/shard_map/all_to_all | solution.py:296
  216.7 19.3 %all-to-all-done.3 = bf16[64,16,384]{2,1,0:T(8,128)(2,1)S(1)} async-done(((bf16[64,16,384]{2,1,0:T(8,128)(2,1)}), bf16[64,16,384]{2,1,0:T(8,128)(2,1)S(1)}, u32[]{:S(2)}, u32[]{:S(2)}) %all-to-all-start.3) | async-done | bytes 786464 | tf_op jit(solution)/shard_map/all_to_all | solution.py:296
  (107 shorter events, 47.4 us)
Async XLA Ops:
  2.7 36.4 %all-to-all-start = ((bf16[64,16,384]{2,1,0:T(8,128)(2,1)}), bf16[64,16,384]{2,1,0:T(8,128)(2,1)S(1)}, u32[]{:S(2)}, u32[]{:S(2)}) async-start(bf16[64,16,384]{2,1,0:T(8,128)(2,1)} %bitcast.42), calls=%async_computation | async-start | bytes 1572864 | tf_op jit(solution)/shard_map/all_to_all | solution.py:296
  17.6 54.4 %collective-permute-start.6 = (bf16[360,2880]{1,0:T(8,128)(2,1)}, bf16[360,2880]{1,0:T(8,128)(2,1)}, u32[]{:S(2)}, u32[]{:S(2)}) collective-permute-start(bf16[360,2880]{1,0:T(8,128)(2,1)} %dynamic-slice_bitcast_fusion.2), channel_id=1, source_target_pairs={{0,1},{1,0},{2,3},{3,2},{4,5},{5,4},{6,7},{7,6},{8,9},{9,8},{10,11... | collective-permute-start | bytes 6220808 | tf_op jit(solution)/shard_map/ppermute | solution.py:309
  19.3 53.0 %collective-permute-start.8 = (bf16[360,2880]{1,0:T(8,128)(2,1)}, bf16[360,2880]{1,0:T(8,128)(2,1)}, u32[]{:S(2)}, u32[]{:S(2)}) collective-permute-start(bf16[360,2880]{1,0:T(8,128)(2,1)} %dynamic-slice_bitcast_fusion), channel_id=1, source_target_pairs={{0,1},{1,0},{2,3},{3,2},{4,5},{5,4},{6,7},{7,6},{8,9},{9,8},{10,11... | collective-permute-start | bytes 6220808 | tf_op jit(solution)/shard_map/ppermute | solution.py:309
  39.0 29.5 %all-to-all-start.2 = ((bf16[64,16,384]{2,1,0:T(8,128)(2,1)}), bf16[64,16,384]{2,1,0:T(8,128)(2,1)S(1)}, u32[]{:S(2)}, u32[]{:S(2)}) async-start(bf16[64,16,384]{2,1,0:T(8,128)(2,1)} %bitcast.41), calls=%async_computation.2 | async-start | bytes 1572864 | tf_op jit(solution)/shard_map/all_to_all | solution.py:296
  46.8 41.0 %collective-permute-start.7 = (bf16[360,2880]{1,0:T(8,128)(2,1)}, bf16[360,2880]{1,0:T(8,128)(2,1)}, u32[]{:S(2)}, u32[]{:S(2)}) collective-permute-start(bf16[360,2880]{1,0:T(8,128)(2,1)} %dynamic-slice_bitcast_fusion.1), channel_id=1, source_target_pairs={{0,1},{1,0},{2,3},{3,2},{4,5},{5,4},{6,7},{7,6},{8,9},{9,8},{10,11... | collective-permute-start | bytes 6220808 | tf_op jit(solution)/shard_map/ppermute | solution.py:309
  47.2 21.5 %collective-permute-start = (bf16[1,512,384]{2,1,0:T(8,128)(2,1)S(1)}, bf16[1,512,384]{2,1,0:T(8,128)(2,1)S(1)}, u32[]{:S(2)}, u32[]{:S(2)}) collective-permute-start(bf16[1,512,384]{2,1,0:T(8,128)(2,1)S(1)} %bitcast.47), channel_id=1, source_target_pairs={{0,2},{2,4},{4,6},{6,0},{1,3},{3,5},{5,7},{7,1},{8,10},{10,12},{12... | collective-permute-start | bytes 1179656 | tf_op jit(solution)/shard_map/ppermute | solution.py:270
  48.8 21.5 %collective-permute-start.1 = (bf16[1,512,384]{2,1,0:T(8,128)(2,1)S(1)}, bf16[1,512,384]{2,1,0:T(8,128)(2,1)S(1)}, u32[]{:S(2)}, u32[]{:S(2)}) collective-permute-start(bf16[1,512,384]{2,1,0:T(8,128)(2,1)S(1)} %bitcast.49), channel_id=1, source_target_pairs={{0,6},{2,0},{4,2},{6,4},{1,7},{3,1},{5,3},{7,5},{8,14},{10,8},{12,... | collective-permute-start | bytes 1179656 | tf_op jit(solution)/shard_map/ppermute | solution.py:270
  68.7 25.3 %collective-permute-start.2 = (bf16[1,512,384]{2,1,0:T(8,128)(2,1)S(1)}, bf16[1,512,384]{2,1,0:T(8,128)(2,1)S(1)}, u32[]{:S(2)}, u32[]{:S(2)}) collective-permute-start(bf16[1,512,384]{2,1,0:T(8,128)(2,1)S(1)} %bitcast.50), channel_id=1, source_target_pairs={{0,2},{2,4},{4,6},{6,0},{1,3},{3,5},{5,7},{7,1},{8,10},{10,12},{12... | collective-permute-start | bytes 1179656 | tf_op jit(solution)/shard_map/ppermute | solution.py:270
  70.3 26.9 %collective-permute-start.3 = (bf16[1,512,384]{2,1,0:T(8,128)(2,1)S(1)}, bf16[1,512,384]{2,1,0:T(8,128)(2,1)S(1)}, u32[]{:S(2)}, u32[]{:S(2)}) collective-permute-start(bf16[1,512,384]{2,1,0:T(8,128)(2,1)S(1)} %bitcast.48), channel_id=1, source_target_pairs={{0,6},{2,0},{4,2},{6,4},{1,7},{3,1},{5,3},{7,5},{8,14},{10,8},{12,... | collective-permute-start | bytes 1179656 | tf_op jit(solution)/shard_map/ppermute | solution.py:270
  72.0 25.2 %collective-permute-start.4 = (bf16[1,512,384]{2,1,0:T(8,128)(2,1)S(1)}, bf16[1,512,384]{2,1,0:T(8,128)(2,1)S(1)}, u32[]{:S(2)}, u32[]{:S(2)}) collective-permute-start(bf16[1,512,384]{2,1,0:T(8,128)(2,1)S(1)} %collective-permute-done.refs_1_), channel_id=1, source_target_pairs={{0,2},{2,4},{4,6},{6,0},{1,3},{3,5},{5,7},{7,1},{8,10},{10,12},{12... | collective-permute-start | bytes 1179656 | tf_op jit(solution)/shard_map/ppermute | solution.py:270
  72.4 24.9 %collective-permute-start.5 = (bf16[1,512,384]{2,1,0:T(8,128)(2,1)S(1)}, bf16[1,512,384]{2,1,0:T(8,128)(2,1)S(1)}, u32[]{:S(2)}, u32[]{:S(2)}) collective-permute-start(bf16[1,512,384]{2,1,0:T(8,128)(2,1)S(1)} %collective-permute-done.1.refs_2_), channel_id=1, source_target_pairs={{0,6},{2,0},{4,2},{6,4},{1,7},{3,1},{5,3},{7,5},{8,14},{10,8},{12,... | collective-permute-start | bytes 1179656 | tf_op jit(solution)/shard_map/ppermute | solution.py:270
  87.8 28.1 %collective-permute-start.15 = (bf16[1,512,384]{2,1,0:T(8,128)(2,1)S(1)}, bf16[1,512,384]{2,1,0:T(8,128)(2,1)S(1)}, u32[]{:S(2)}, u32[]{:S(2)}) collective-permute-start(bf16[1,512,384]{2,1,0:T(8,128)(2,1)S(1)} %bitcast.43), channel_id=1, source_target_pairs={{0,2},{2,4},{4,6},{6,0},{1,3},{3,5},{5,7},{7,1},{8,10},{10,12},{12... | collective-permute-start | bytes 1179656 | tf_op jit(solution)/shard_map/ppermute | solution.py:270
  94.0 25.1 %collective-permute-start.16 = (bf16[1,512,384]{2,1,0:T(8,128)(2,1)S(1)}, bf16[1,512,384]{2,1,0:T(8,128)(2,1)S(1)}, u32[]{:S(2)}, u32[]{:S(2)}) collective-permute-start(bf16[1,512,384]{2,1,0:T(8,128)(2,1)S(1)} %bitcast.45), channel_id=1, source_target_pairs={{0,6},{2,0},{4,2},{6,4},{1,7},{3,1},{5,3},{7,5},{8,14},{10,8},{12,... | collective-permute-start | bytes 1179656 | tf_op jit(solution)/shard_map/ppermute | solution.py:270
  115.9 20.0 %collective-permute-start.17 = (bf16[1,512,384]{2,1,0:T(8,128)(2,1)S(1)}, bf16[1,512,384]{2,1,0:T(8,128)(2,1)S(1)}, u32[]{:S(2)}, u32[]{:S(2)}) collective-permute-start(bf16[1,512,384]{2,1,0:T(8,128)(2,1)S(1)} %bitcast.46), channel_id=1, source_target_pairs={{0,2},{2,4},{4,6},{6,0},{1,3},{3,5},{5,7},{7,1},{8,10},{10,12},{12... | collective-permute-start | bytes 1179656 | tf_op jit(solution)/shard_map/ppermute | solution.py:270
  115.9 19.9 %collective-permute-start.18 = (bf16[1,512,384]{2,1,0:T(8,128)(2,1)S(1)}, bf16[1,512,384]{2,1,0:T(8,128)(2,1)S(1)}, u32[]{:S(2)}, u32[]{:S(2)}) collective-permute-start(bf16[1,512,384]{2,1,0:T(8,128)(2,1)S(1)} %bitcast.44), channel_id=1, source_target_pairs={{0,6},{2,0},{4,2},{6,4},{1,7},{3,1},{5,3},{7,5},{8,14},{10,8},{12,... | collective-permute-start | bytes 1179656 | tf_op jit(solution)/shard_map/ppermute | solution.py:270
  119.1 25.1 %collective-permute-start.19 = (bf16[1,512,384]{2,1,0:T(8,128)(2,1)S(1)}, bf16[1,512,384]{2,1,0:T(8,128)(2,1)S(1)}, u32[]{:S(2)}, u32[]{:S(2)}) collective-permute-start(bf16[1,512,384]{2,1,0:T(8,128)(2,1)S(1)} %collective-permute-done.15.refs_1_), channel_id=1, source_target_pairs={{0,2},{2,4},{4,6},{6,0},{1,3},{3,5},{5,7},{7,1},{8,10},{10,12},{12... | collective-permute-start | bytes 1179656 | tf_op jit(solution)/shard_map/ppermute | solution.py:270
  126.1 18.9 %collective-permute-start.20 = (bf16[1,512,384]{2,1,0:T(8,128)(2,1)S(1)}, bf16[1,512,384]{2,1,0:T(8,128)(2,1)S(1)}, u32[]{:S(2)}, u32[]{:S(2)}) collective-permute-start(bf16[1,512,384]{2,1,0:T(8,128)(2,1)S(1)} %collective-permute-done.16.refs_2_), channel_id=1, source_target_pairs={{0,6},{2,0},{4,2},{6,4},{1,7},{3,1},{5,3},{7,5},{8,14},{10,8},{12,... | collective-permute-start | bytes 1179656 | tf_op jit(solution)/shard_map/ppermute | solution.py:270
  128.5 35.5 %collective-permute-start.12 = (bf16[1,512,384]{2,1,0:T(8,128)(2,1)}, bf16[1,512,384]{2,1,0:T(8,128)(2,1)S(1)}, u32[]{:S(2)}, u32[]{:S(2)}) collective-permute-start(bf16[1,512,384]{2,1,0:T(8,128)(2,1)} %get-tuple-element.23), channel_id=1, source_target_pairs={{0,2},{2,4},{4,6},{6,0},{1,3},{3,5},{5,7},{7,1},{8,10},{10,12},{12... | collective-permute-start | bytes 1179656 | tf_op jit(solution)/shard_map/ppermute | solution.py:270
  135.8 28.2 %collective-permute-start.9 = (bf16[1,512,384]{2,1,0:T(8,128)(2,1)}, bf16[1,512,384]{2,1,0:T(8,128)(2,1)S(1)}, u32[]{:S(2)}, u32[]{:S(2)}) collective-permute-start(bf16[1,512,384]{2,1,0:T(8,128)(2,1)} %get-tuple-element.20), channel_id=1, source_target_pairs={{0,6},{2,0},{4,2},{6,4},{1,7},{3,1},{5,3},{7,5},{8,14},{10,8},{12,... | collective-permute-start | bytes 1179656 | tf_op jit(solution)/shard_map/ppermute | solution.py:270
  135.9 28.2 %collective-permute-start.14 = (bf16[1,512,384]{2,1,0:T(8,128)(2,1)S(1)}, bf16[1,512,384]{2,1,0:T(8,128)(2,1)S(1)}, u32[]{:S(2)}, u32[]{:S(2)}) collective-permute-start(bf16[1,512,384]{2,1,0:T(8,128)(2,1)S(1)} %add_convert_fusion.5), channel_id=1, source_target_pairs={{0,6},{2,0},{4,2},{6,4},{1,7},{3,1},{5,3},{7,5},{8,14},{10,8},{12,... | collective-permute-start | bytes 1179656 | tf_op jit(solution)/shard_map/ppermute | solution.py:270
  144.3 19.8 %collective-permute-start.11 = (bf16[1,512,384]{2,1,0:T(8,128)(2,1)S(1)}, bf16[1,512,384]{2,1,0:T(8,128)(2,1)S(1)}, u32[]{:S(2)}, u32[]{:S(2)}) collective-permute-start(bf16[1,512,384]{2,1,0:T(8,128)(2,1)S(1)} %add_convert_fusion.7), channel_id=1, source_target_pairs={{0,2},{2,4},{4,6},{6,0},{1,3},{3,5},{5,7},{7,1},{8,10},{10,12},{12... | collective-permute-start | bytes 1179656 | tf_op jit(solution)/shard_map/ppermute | solution.py:270
  165.4 35.6 %all-to-all-start.1 = ((bf16[64,16,384]{2,1,0:T(8,128)(2,1)}), bf16[64,16,384]{2,1,0:T(8,128)(2,1)S(1)}, u32[]{:S(2)}, u32[]{:S(2)}) async-start(bf16[64,16,384]{2,1,0:T(8,128)(2,1)} %bitcast.15), calls=%async_computation.1 | async-start | bytes 1572864 | tf_op jit(solution)/shard_map/all_to_all | solution.py:296
  173.3 18.6 %collective-permute-start.24 = (bf16[1,512,384]{2,1,0:T(8,128)(2,1)S(1)}, bf16[1,512,384]{2,1,0:T(8,128)(2,1)S(1)}, u32[]{:S(2)}, u32[]{:S(2)}) collective-permute-start(bf16[1,512,384]{2,1,0:T(8,128)(2,1)S(1)} %copy-done.19), channel_id=1, source_target_pairs={{0,2},{2,4},{4,6},{6,0},{1,3},{3,5},{5,7},{7,1},{8,10},{10,12},{12... | collective-permute-start | bytes 1179656 | tf_op jit(solution)/shard_map/ppermute | solution.py:270
  201.0 35.1 %all-to-all-start.3 = ((bf16[64,16,384]{2,1,0:T(8,128)(2,1)}), bf16[64,16,384]{2,1,0:T(8,128)(2,1)S(1)}, u32[]{:S(2)}, u32[]{:S(2)}) async-start(bf16[64,16,384]{2,1,0:T(8,128)(2,1)} %bitcast.22), calls=%async_computation.3 | async-start | bytes 1572864 | tf_op jit(solution)/shard_map/all_to_all | solution.py:296
  (28 other events, 350.1 us)

commit v3 on v2

--- a/solution.py
+++ b/solution.py
@@ -46,22 +46,17 @@
 def dispatch(ids_t, tok_t, experts, start, size):
     feats, toks = tok_t.shape
 
-    def body(ids_ref, tok_ref, out_ref, pad_ref, rank_ref):
-        pad_ref[...] = jnp.zeros(pad_ref.shape, bf16)
+    def body(ids_ref, tok_ref, out_ref, pad_ref):
         pad_ref[:feats, :] = tok_ref[...]
-        rank_ref[...] = slots_of(ids_ref[...], experts)[1]
-
-        @pl.loop(0, experts // GROUP)
-        def _(i):
-            rank = rank_ref[pl.ds(pl.multiple_of(i * GROUP, GROUP), GROUP), :]
-            pick = spread(rank, start, size).astype(f32).reshape(GROUP * size, toks).astype(bf16)
-            rows = lax.dot_general(pick, pad_ref[...], NT, preferred_element_type=f32)
-            out_ref[pl.ds(pl.multiple_of(i * GROUP * size, GROUP * size), GROUP * size), :] = rows.astype(bf16)
+        pad_ref[feats:, :] = jnp.zeros((LANES - feats, toks), bf16)
+        _, rank = slots_of(ids_ref[...], experts)
+        pick = spread(rank, start, size).astype(f32).reshape(experts * size, toks).astype(bf16)
+        out_ref[...] = lax.dot_general(pick, pad_ref[...], NT, preferred_element_type=f32).astype(bf16)
 
     return pl.pallas_call(
         body,
         out_shape=jax.ShapeDtypeStruct((experts * size, LANES), bf16),
-        scratch_shapes=[pltpu.VMEM((LANES, toks), bf16), pltpu.VMEM((experts, toks), f32)],
+        scratch_shapes=[pltpu.VMEM((LANES, toks), bf16)],
         compiler_params=pltpu.CompilerParams(vmem_limit_bytes=VMEM),
         cost_estimate=lasting(3),
     )(ids_t, tok_t)

time: 240 us -> 240 us (level)
  no operation moved by 1% of the time
where the time goes in v3:
time: 240 us; the launch traced here: 238 us
  waiting for transfers between devices  96.8 us (40%)
  starting transfers between devices  63.7 us (27%)
  Pallas kernels  58.7 us (24%)
  local copies, waits for them, and re-layouts  9.86 us (4%)
  other arithmetic  5.69 us (2%)
  matrix products  2.9 us (1%)
    all_to_all x4, waiting for transfers between devices, exchange(): return lax.all_to_all(array, ('c', 'x', 'z'), 0, 0, tiled=True)  54.4 us
    ppermute x24, waiting for transfers between devices, shift(): return lax.ppermute(array, 'y', [(i, (i + by) % RING) for i in range(RING)])  42.4 us
    ppermute x24, starting transfers between devices, shift(): return lax.ppermute(array, 'y', [(i, (i + by) % RING) for i in range(RING)])  31.8 us
    pallas_call x4, Pallas kernels, kernel(): pl.pallas_call(body, in_specs=[pl.BlockSpec(memory_space=pltpu.MemorySpac...  31.2 us
    all_to_all x4, starting transfers between devices, exchange(): return lax.all_to_all(array, ('c', 'x', 'z'), 0, 0, tiled=True)  31.1 us
    pallas_call x3, Pallas kernels, arrange(): pl.pallas_call(body, grid_spec=pltpu.PrefetchScalarGridSpec(num_scalar_pr...  18.7 us
    squeeze x3, local copies, waits for them, and re-layouts, local(): other = lax.dynamic_index_in_dim(w, 1 - core, 0, keepdims=False)  7.94 us
    pallas_call x2, Pallas kernels, dispatch(): pl.pallas_call(body, out_shape=jax.ShapeDtypeStruct((experts * size, LANE...  4.85 us
  transfers between devices with their start and end apart: 31, of which 9 were waited for; matrix products, arithmetic and copies ran while one was open for 6% of the time, Pallas kernels for 24%

profile of v3, /device:TPU:32, one launch (start us, length us, event | category | flops | bytes accessed | tf_op | source)
XLA Modules:
  0.0 238.0 jit_solution(6463484418867601488)
XLA Ops:
  2.4 11.6 %all-to-all-start = ((bf16[64,16,384]{2,1,0:T(8,128)(2,1)}), bf16[64,16,384]{2,1,0:T(8,128)(2,1)S(1)}, u32[]{:S(2)}, u32[]{:S(2)}) async-start(bf16[64,16,384]{2,1,0:T(8,128)(2,1)} %bitcast.42), calls=%async_computation | async-start | bytes 1572864 | tf_op jit(solution)/shard_map/all_to_all | solution.py:291
  14.0 3.3 %dynamic-slice_bitcast_fusion.2 = bf16[360,2880]{1,0:T(8,128)(2,1)} fusion(bf16[2,2880,360]{1,2,0:T(8,128)(2,1)} %param.9, s32[]{:T(128)S(6)} %select_n.6), kind=kLoop, calls=%fused_computation.2 | loop fusion | bytes 4147204 | tf_op jit(solution)/shard_map/jit(dynamic_index_in_dim)/squeeze | solution.py:303
  21.8 17.0 %all-to-all-done = bf16[64,16,384]{2,1,0:T(8,128)(2,1)S(1)} async-done(((bf16[64,16,384]{2,1,0:T(8,128)(2,1)}), bf16[64,16,384]{2,1,0:T(8,128)(2,1)S(1)}, u32[]{:S(2)}, u32[]{:S(2)}) %all-to-all-start) | async-done | bytes 786464 | tf_op jit(solution)/shard_map/all_to_all | solution.py:291
  38.8 4.6 %all-to-all-start.2 = ((bf16[64,16,384]{2,1,0:T(8,128)(2,1)}), bf16[64,16,384]{2,1,0:T(8,128)(2,1)S(1)}, u32[]{:S(2)}, u32[]{:S(2)}) async-start(bf16[64,16,384]{2,1,0:T(8,128)(2,1)} %bitcast.41), calls=%async_computation.2 | async-start | bytes 1572864 | tf_op jit(solution)/shard_map/all_to_all | solution.py:291
  50.2 18.1 %all-to-all-done.2 = bf16[64,16,384]{2,1,0:T(8,128)(2,1)S(1)} async-done(((bf16[64,16,384]{2,1,0:T(8,128)(2,1)}), bf16[64,16,384]{2,1,0:T(8,128)(2,1)S(1)}, u32[]{:S(2)}, u32[]{:S(2)}) %all-to-all-start.2) | async-done | bytes 786464 | tf_op jit(solution)/shard_map/all_to_all | solution.py:291
  75.0 6.2 %arrange.5.w_ref = bf16[4,736,768]{2,1,0:T(8,128)(2,1)} custom-call(s32[1]{0:T(128)} %bitcast.7.core_ref, bf16[2,360,2880]{2,1,0:T(8,128)(2,1)} %own_ref.1, bf16[360,2880]{1,0:T(8,128)(2,1)} %collective-permute-done.8.recv_ref), custom_call_target="tpu_custom_call" | custom-call | flops 1500000000 | tf_op jit(solution)/shard_map/arrange/pallas_call | solution.py:120
  81.2 6.3 %arrange.3.refs_7_ = bf16[4,736,768]{2,1,0:T(8,128)(2,1)} custom-call(s32[1]{0:T(128)} %bitcast.7.core_ref, bf16[2,360,2880]{2,1,0:T(8,128)(2,1)} %bitcast.35, bf16[360,2880]{1,0:T(8,128)(2,1)} %collective-permute-done.6.recv_ref), custom_call_target="tpu_custom_call" | custom-call | flops 1500000000 | tf_op jit(solution)/shard_map/arrange/pallas_call | solution.py:120
  87.5 6.2 %arrange.4.refs_8_ = bf16[4,736,768]{2,1,0:T(8,128)(2,1)} custom-call(s32[1]{0:T(128)} %bitcast.7.core_ref, bf16[2,360,2880]{2,1,0:T(8,128)(2,1)} %bitcast.36, bf16[360,2880]{1,0:T(8,128)(2,1)} %collective-permute-done.7.recv_ref), custom_call_target="tpu_custom_call" | custom-call | flops 1500000000 | tf_op jit(solution)/shard_map/arrange/pallas_call | solution.py:120
  98.0 9.5 %shard_map.65.hid_ref = bf16[512,736]{1,0:T(8,128)(2,1)} custom-call(s32[1]{0:T(128)} %bitcast.row_ref, bf16[2,512,384]{2,1,0:T(8,128)(2,1)} %bitcast.38, bf16[1,512,384]{2,1,0:T(8,128)(2,1)} %copy-done.7, bf16[1,512,384]{2,1,0:T(8,128)(2,1)} %copy-done.8, bf16[1,512,384]{2,1,0:T(8,128)(2,1)} %copy-done.11, bf16[1,512,384]{2,1,0:T(8,128)(2,1)} %copy-done.13, ...), custom_call_target="tpu_custom_call" | custom-call | flops 2249999872 | tf_op jit(solution)/shard_map/pallas_call | solution.py:155
  107.5 6.1 %shard_map.66 = (bf16[2,512,384]{2,1,0:T(8,128)(2,1)}, bf16[1,512,384]{2,1,0:T(8,128)(2,1)}, bf16[1,512,384]{2,1,0:T(8,128)(2,1)}, bf16[1,512,384]{2,1,0:T(8,128...) custom-call(s32[1]{0:T(128)} %bitcast.row_ref, ...), custom_call_target="tpu_custom_call" | custom-call | flops 1250000000 | tf_op jit(solution)/shard_map/pallas_call | solution.py:155
  115.7 3.2 %collective-permute-start.18 = (bf16[1,512,384]{2,1,0:T(8,128)(2,1)S(1)}, bf16[1,512,384]{2,1,0:T(8,128)(2,1)S(1)}, u32[]{:S(2)}, u32[]{:S(2)}) collective-permute-start(bf16[1,512,384]{2,1,0:T(8,128)(2,1)S(1)} %bitcast.44), channel_id=1, source_target_pairs={{0,6},{2,0},{4,2},{6,4},{1,7},{3,1},{5,3},{7,5},{8,14},{10,8},{12,... | collective-permute-start | bytes 1179656 | tf_op jit(solution)/shard_map/ppermute | solution.py:265
  118.9 6.9 %collective-permute-done.13 = bf16[1,512,384]{2,1,0:T(8,128)(2,1)S(1)} collective-permute-done((bf16[1,512,384]{2,1,0:T(8,128)(2,1)}, bf16[1,512,384]{2,1,0:T(8,128)(2,1)S(1)}, u32[]{:S(2)}, u32[]{:S(2)}) %collective-permute-start.13) | collective-permute-done | bytes 393248 | tf_op jit(solution)/shard_map/ppermute | solution.py:265
  130.1 5.5 %collective-permute-done.17.refs_3_ = bf16[1,512,384]{2,1,0:T(8,128)(2,1)S(1)} collective-permute-done((bf16[1,512,384]{2,1,0:T(8,128)(2,1)S(1)}, bf16[1,512,384]{2,1,0:T(8,128)(2,1)S(1)}, u32[]{:S(2)}, u32[]{:S(2)}) %collective-permute-start.17) | collective-permute-done | bytes 393248 | tf_op jit(solution)/shard_map/ppermute | solution.py:265
  136.9 7.2 %collective-permute-done.19.refs_5_ = bf16[1,512,384]{2,1,0:T(8,128)(2,1)S(1)} collective-permute-done((bf16[1,512,384]{2,1,0:T(8,128)(2,1)S(1)}, bf16[1,512,384]{2,1,0:T(8,128)(2,1)S(1)}, u32[]{:S(2)}, u32[]{:S(2)}) %collective-permute-start.19) | collective-permute-done | bytes 393248 | tf_op jit(solution)/shard_map/ppermute | solution.py:265
  145.4 9.5 %shard_map.69.hid_ref = bf16[512,736]{1,0:T(8,128)(2,1)} custom-call(s32[1]{0:T(128)} %bitcast.row_ref, bf16[2,512,384]{2,1,0:T(8,128)(2,1)} %bitcast.37, bf16[1,512,384]{2,1,0:T(8,128)(2,1)} %copy-done.5, bf16[1,512,384]{2,1,0:T(8,128)(2,1)} %copy-done.6, bf16[1,512,384]{2,1,0:T(8,128)(2,1)} %copy-done.9, bf16[1,512,384]{2,1,0:T(8,128)(2,1)} %copy-done.10, ...), custom_call_target="tpu_custom_call" | custom-call | flops 2249999872 | tf_op jit(solution)/shard_map/pallas_call | solution.py:155
  154.9 6.2 %shard_map.70 = (bf16[2,512,384]{2,1,0:T(8,128)(2,1)}, bf16[1,512,384]{2,1,0:T(8,128)(2,1)}, bf16[1,512,384]{2,1,0:T(8,128)(2,1)}, bf16[1,512,384]{2,1,0:T(8,128...) custom-call(s32[1]{0:T(128)} %bitcast.row_ref, ...), custom_call_target="tpu_custom_call" | custom-call | flops 1250000000 | tf_op jit(solution)/shard_map/pallas_call | solution.py:155
  165.1 4.6 %all-to-all-start.1 = ((bf16[64,16,384]{2,1,0:T(8,128)(2,1)}), bf16[64,16,384]{2,1,0:T(8,128)(2,1)S(1)}, u32[]{:S(2)}, u32[]{:S(2)}) async-start(bf16[64,16,384]{2,1,0:T(8,128)(2,1)} %bitcast.15), calls=%async_computation.1 | async-start | bytes 1572864 | tf_op jit(solution)/shard_map/all_to_all | solution.py:291
  169.9 3.2 %collective-permute-start.21 = (bf16[1,512,384]{2,1,0:T(8,128)(2,1)S(1)}, bf16[1,512,384]{2,1,0:T(8,128)(2,1)S(1)}, u32[]{:S(2)}, u32[]{:S(2)}) collective-permute-start(bf16[1,512,384]{2,1,0:T(8,128)(2,1)S(1)} %copy-done.20), channel_id=1, source_target_pairs={{0,6},{2,0},{4,2},{6,4},{1,7},{3,1},{5,3},{7,5},{8,14},{10,8},{12,... | collective-permute-start | bytes 1179656 | tf_op jit(solution)/shard_map/ppermute | solution.py:265
  173.2 3.3 %collective-permute-start.26 = (bf16[1,512,384]{2,1,0:T(8,128)(2,1)S(1)}, bf16[1,512,384]{2,1,0:T(8,128)(2,1)S(1)}, u32[]{:S(2)}, u32[]{:S(2)}) collective-permute-start(bf16[1,512,384]{2,1,0:T(8,128)(2,1)S(1)} %add_convert_fusion.1), channel_id=1, source_target_pairs={{0,6},{2,0},{4,2},{6,4},{1,7},{3,1},{5,3},{7,5},{8,14},{10,8},{12,... | collective-permute-start | bytes 1179656 | tf_op jit(solution)/shard_map/ppermute | solution.py:265
  176.5 6.7 %collective-permute-done.22 = bf16[1,512,384]{2,1,0:T(8,128)(2,1)S(1)} collective-permute-done((bf16[1,512,384]{2,1,0:T(8,128)(2,1)}, bf16[1,512,384]{2,1,0:T(8,128)(2,1)S(1)}, u32[]{:S(2)}, u32[]{:S(2)}) %collective-permute-start.22) | collective-permute-done | bytes 393248 | tf_op jit(solution)/shard_map/ppermute | solution.py:265
  183.4 8.2 %collective-permute-done.24 = bf16[1,512,384]{2,1,0:T(8,128)(2,1)S(1)} collective-permute-done((bf16[1,512,384]{2,1,0:T(8,128)(2,1)S(1)}, bf16[1,512,384]{2,1,0:T(8,128)(2,1)S(1)}, u32[]{:S(2)}, u32[]{:S(2)}) %collective-permute-start.24) | collective-permute-done | bytes 393248 | tf_op jit(solution)/shard_map/ppermute | solution.py:265
  191.7 7.8 %collective-permute-done.23 = bf16[1,512,384]{2,1,0:T(8,128)(2,1)S(1)} collective-permute-done((bf16[1,512,384]{2,1,0:T(8,128)(2,1)S(1)}, bf16[1,512,384]{2,1,0:T(8,128)(2,1)S(1)}, u32[]{:S(2)}, u32[]{:S(2)}) %collective-permute-start.23) | collective-permute-done | bytes 393248 | tf_op jit(solution)/shard_map/ppermute | solution.py:265
  200.8 10.3 %all-to-all-start.3 = ((bf16[64,16,384]{2,1,0:T(8,128)(2,1)}), bf16[64,16,384]{2,1,0:T(8,128)(2,1)S(1)}, u32[]{:S(2)}, u32[]{:S(2)}) async-start(bf16[64,16,384]{2,1,0:T(8,128)(2,1)} %bitcast.22), calls=%async_computation.3 | async-start | bytes 1572864 | tf_op jit(solution)/shard_map/all_to_all | solution.py:291
  216.5 19.3 %all-to-all-done.3 = bf16[64,16,384]{2,1,0:T(8,128)(2,1)S(1)} async-done(((bf16[64,16,384]{2,1,0:T(8,128)(2,1)}), bf16[64,16,384]{2,1,0:T(8,128)(2,1)S(1)}, u32[]{:S(2)}, u32[]{:S(2)}) %all-to-all-start.3) | async-done | bytes 786464 | tf_op jit(solution)/shard_map/all_to_all | solution.py:291
  (107 shorter events, 46.9 us)
Async XLA Ops:
  2.4 36.4 %all-to-all-start = ((bf16[64,16,384]{2,1,0:T(8,128)(2,1)}), bf16[64,16,384]{2,1,0:T(8,128)(2,1)S(1)}, u32[]{:S(2)}, u32[]{:S(2)}) async-start(bf16[64,16,384]{2,1,0:T(8,128)(2,1)} %bitcast.42), calls=%async_computation | async-start | bytes 1572864 | tf_op jit(solution)/shard_map/all_to_all | solution.py:291
  17.3 54.4 %collective-permute-start.6 = (bf16[360,2880]{1,0:T(8,128)(2,1)}, bf16[360,2880]{1,0:T(8,128)(2,1)}, u32[]{:S(2)}, u32[]{:S(2)}) collective-permute-start(bf16[360,2880]{1,0:T(8,128)(2,1)} %dynamic-slice_bitcast_fusion.2), channel_id=1, source_target_pairs={{0,1},{1,0},{2,3},{3,2},{4,5},{5,4},{6,7},{7,6},{8,9},{9,8},{10,11... | collective-permute-start | bytes 6220808 | tf_op jit(solution)/shard_map/ppermute | solution.py:304
  19.1 53.0 %collective-permute-start.8 = (bf16[360,2880]{1,0:T(8,128)(2,1)}, bf16[360,2880]{1,0:T(8,128)(2,1)}, u32[]{:S(2)}, u32[]{:S(2)}) collective-permute-start(bf16[360,2880]{1,0:T(8,128)(2,1)} %dynamic-slice_bitcast_fusion), channel_id=1, source_target_pairs={{0,1},{1,0},{2,3},{3,2},{4,5},{5,4},{6,7},{7,6},{8,9},{9,8},{10,11... | collective-permute-start | bytes 6220808 | tf_op jit(solution)/shard_map/ppermute | solution.py:304
  38.8 29.5 %all-to-all-start.2 = ((bf16[64,16,384]{2,1,0:T(8,128)(2,1)}), bf16[64,16,384]{2,1,0:T(8,128)(2,1)S(1)}, u32[]{:S(2)}, u32[]{:S(2)}) async-start(bf16[64,16,384]{2,1,0:T(8,128)(2,1)} %bitcast.41), calls=%async_computation.2 | async-start | bytes 1572864 | tf_op jit(solution)/shard_map/all_to_all | solution.py:291
  46.5 41.0 %collective-permute-start.7 = (bf16[360,2880]{1,0:T(8,128)(2,1)}, bf16[360,2880]{1,0:T(8,128)(2,1)}, u32[]{:S(2)}, u32[]{:S(2)}) collective-permute-start(bf16[360,2880]{1,0:T(8,128)(2,1)} %dynamic-slice_bitcast_fusion.1), channel_id=1, source_target_pairs={{0,1},{1,0},{2,3},{3,2},{4,5},{5,4},{6,7},{7,6},{8,9},{9,8},{10,11... | collective-permute-start | bytes 6220808 | tf_op jit(solution)/shard_map/ppermute | solution.py:304
  46.9 21.5 %collective-permute-start = (bf16[1,512,384]{2,1,0:T(8,128)(2,1)S(1)}, bf16[1,512,384]{2,1,0:T(8,128)(2,1)S(1)}, u32[]{:S(2)}, u32[]{:S(2)}) collective-permute-start(bf16[1,512,384]{2,1,0:T(8,128)(2,1)S(1)} %bitcast.47), channel_id=1, source_target_pairs={{0,2},{2,4},{4,6},{6,0},{1,3},{3,5},{5,7},{7,1},{8,10},{10,12},{12... | collective-permute-start | bytes 1179656 | tf_op jit(solution)/shard_map/ppermute | solution.py:265
  48.6 21.5 %collective-permute-start.1 = (bf16[1,512,384]{2,1,0:T(8,128)(2,1)S(1)}, bf16[1,512,384]{2,1,0:T(8,128)(2,1)S(1)}, u32[]{:S(2)}, u32[]{:S(2)}) collective-permute-start(bf16[1,512,384]{2,1,0:T(8,128)(2,1)S(1)} %bitcast.49), channel_id=1, source_target_pairs={{0,6},{2,0},{4,2},{6,4},{1,7},{3,1},{5,3},{7,5},{8,14},{10,8},{12,... | collective-permute-start | bytes 1179656 | tf_op jit(solution)/shard_map/ppermute | solution.py:265
  68.4 25.3 %collective-permute-start.2 = (bf16[1,512,384]{2,1,0:T(8,128)(2,1)S(1)}, bf16[1,512,384]{2,1,0:T(8,128)(2,1)S(1)}, u32[]{:S(2)}, u32[]{:S(2)}) collective-permute-start(bf16[1,512,384]{2,1,0:T(8,128)(2,1)S(1)} %bitcast.50), channel_id=1, source_target_pairs={{0,2},{2,4},{4,6},{6,0},{1,3},{3,5},{5,7},{7,1},{8,10},{10,12},{12... | collective-permute-start | bytes 1179656 | tf_op jit(solution)/shard_map/ppermute | solution.py:265
  70.1 26.9 %collective-permute-start.3 = (bf16[1,512,384]{2,1,0:T(8,128)(2,1)S(1)}, bf16[1,512,384]{2,1,0:T(8,128)(2,1)S(1)}, u32[]{:S(2)}, u32[]{:S(2)}) collective-permute-start(bf16[1,512,384]{2,1,0:T(8,128)(2,1)S(1)} %bitcast.48), channel_id=1, source_target_pairs={{0,6},{2,0},{4,2},{6,4},{1,7},{3,1},{5,3},{7,5},{8,14},{10,8},{12,... | collective-permute-start | bytes 1179656 | tf_op jit(solution)/shard_map/ppermute | solution.py:265
  71.7 25.2 %collective-permute-start.4 = (bf16[1,512,384]{2,1,0:T(8,128)(2,1)S(1)}, bf16[1,512,384]{2,1,0:T(8,128)(2,1)S(1)}, u32[]{:S(2)}, u32[]{:S(2)}) collective-permute-start(bf16[1,512,384]{2,1,0:T(8,128)(2,1)S(1)} %collective-permute-done.refs_1_), channel_id=1, source_target_pairs={{0,2},{2,4},{4,6},{6,0},{1,3},{3,5},{5,7},{7,1},{8,10},{10,12},{12... | collective-permute-start | bytes 1179656 | tf_op jit(solution)/shard_map/ppermute | solution.py:265
  72.1 24.9 %collective-permute-start.5 = (bf16[1,512,384]{2,1,0:T(8,128)(2,1)S(1)}, bf16[1,512,384]{2,1,0:T(8,128)(2,1)S(1)}, u32[]{:S(2)}, u32[]{:S(2)}) collective-permute-start(bf16[1,512,384]{2,1,0:T(8,128)(2,1)S(1)} %collective-permute-done.1.refs_2_), channel_id=1, source_target_pairs={{0,6},{2,0},{4,2},{6,4},{1,7},{3,1},{5,3},{7,5},{8,14},{10,8},{12,... | collective-permute-start | bytes 1179656 | tf_op jit(solution)/shard_map/ppermute | solution.py:265
  87.5 28.1 %collective-permute-start.15 = (bf16[1,512,384]{2,1,0:T(8,128)(2,1)S(1)}, bf16[1,512,384]{2,1,0:T(8,128)(2,1)S(1)}, u32[]{:S(2)}, u32[]{:S(2)}) collective-permute-start(bf16[1,512,384]{2,1,0:T(8,128)(2,1)S(1)} %bitcast.43), channel_id=1, source_target_pairs={{0,2},{2,4},{4,6},{6,0},{1,3},{3,5},{5,7},{7,1},{8,10},{10,12},{12... | collective-permute-start | bytes 1179656 | tf_op jit(solution)/shard_map/ppermute | solution.py:265
  93.7 25.1 %collective-permute-start.16 = (bf16[1,512,384]{2,1,0:T(8,128)(2,1)S(1)}, bf16[1,512,384]{2,1,0:T(8,128)(2,1)S(1)}, u32[]{:S(2)}, u32[]{:S(2)}) collective-permute-start(bf16[1,512,384]{2,1,0:T(8,128)(2,1)S(1)} %bitcast.45), channel_id=1, source_target_pairs={{0,6},{2,0},{4,2},{6,4},{1,7},{3,1},{5,3},{7,5},{8,14},{10,8},{12,... | collective-permute-start | bytes 1179656 | tf_op jit(solution)/shard_map/ppermute | solution.py:265
  115.6 20.0 %collective-permute-start.17 = (bf16[1,512,384]{2,1,0:T(8,128)(2,1)S(1)}, bf16[1,512,384]{2,1,0:T(8,128)(2,1)S(1)}, u32[]{:S(2)}, u32[]{:S(2)}) collective-permute-start(bf16[1,512,384]{2,1,0:T(8,128)(2,1)S(1)} %bitcast.46), channel_id=1, source_target_pairs={{0,2},{2,4},{4,6},{6,0},{1,3},{3,5},{5,7},{7,1},{8,10},{10,12},{12... | collective-permute-start | bytes 1179656 | tf_op jit(solution)/shard_map/ppermute | solution.py:265
  115.7 19.9 %collective-permute-start.18 = (bf16[1,512,384]{2,1,0:T(8,128)(2,1)S(1)}, bf16[1,512,384]{2,1,0:T(8,128)(2,1)S(1)}, u32[]{:S(2)}, u32[]{:S(2)}) collective-permute-start(bf16[1,512,384]{2,1,0:T(8,128)(2,1)S(1)} %bitcast.44), channel_id=1, source_target_pairs={{0,6},{2,0},{4,2},{6,4},{1,7},{3,1},{5,3},{7,5},{8,14},{10,8},{12,... | collective-permute-start | bytes 1179656 | tf_op jit(solution)/shard_map/ppermute | solution.py:265
  118.9 25.1 %collective-permute-start.19 = (bf16[1,512,384]{2,1,0:T(8,128)(2,1)S(1)}, bf16[1,512,384]{2,1,0:T(8,128)(2,1)S(1)}, u32[]{:S(2)}, u32[]{:S(2)}) collective-permute-start(bf16[1,512,384]{2,1,0:T(8,128)(2,1)S(1)} %collective-permute-done.15.refs_1_), channel_id=1, source_target_pairs={{0,2},{2,4},{4,6},{6,0},{1,3},{3,5},{5,7},{7,1},{8,10},{10,12},{12... | collective-permute-start | bytes 1179656 | tf_op jit(solution)/shard_map/ppermute | solution.py:265
  125.8 18.9 %collective-permute-start.20 = (bf16[1,512,384]{2,1,0:T(8,128)(2,1)S(1)}, bf16[1,512,384]{2,1,0:T(8,128)(2,1)S(1)}, u32[]{:S(2)}, u32[]{:S(2)}) collective-permute-start(bf16[1,512,384]{2,1,0:T(8,128)(2,1)S(1)} %collective-permute-done.16.refs_2_), channel_id=1, source_target_pairs={{0,6},{2,0},{4,2},{6,4},{1,7},{3,1},{5,3},{7,5},{8,14},{10,8},{12,... | collective-permute-start | bytes 1179656 | tf_op jit(solution)/shard_map/ppermute | solution.py:265
  128.3 35.5 %collective-permute-start.12 = (bf16[1,512,384]{2,1,0:T(8,128)(2,1)}, bf16[1,512,384]{2,1,0:T(8,128)(2,1)S(1)}, u32[]{:S(2)}, u32[]{:S(2)}) collective-permute-start(bf16[1,512,384]{2,1,0:T(8,128)(2,1)} %get-tuple-element.23), channel_id=1, source_target_pairs={{0,2},{2,4},{4,6},{6,0},{1,3},{3,5},{5,7},{7,1},{8,10},{10,12},{12... | collective-permute-start | bytes 1179656 | tf_op jit(solution)/shard_map/ppermute | solution.py:265
  135.6 28.2 %collective-permute-start.9 = (bf16[1,512,384]{2,1,0:T(8,128)(2,1)}, bf16[1,512,384]{2,1,0:T(8,128)(2,1)S(1)}, u32[]{:S(2)}, u32[]{:S(2)}) collective-permute-start(bf16[1,512,384]{2,1,0:T(8,128)(2,1)} %get-tuple-element.20), channel_id=1, source_target_pairs={{0,6},{2,0},{4,2},{6,4},{1,7},{3,1},{5,3},{7,5},{8,14},{10,8},{12,... | collective-permute-start | bytes 1179656 | tf_op jit(solution)/shard_map/ppermute | solution.py:265
  135.6 28.2 %collective-permute-start.14 = (bf16[1,512,384]{2,1,0:T(8,128)(2,1)S(1)}, bf16[1,512,384]{2,1,0:T(8,128)(2,1)S(1)}, u32[]{:S(2)}, u32[]{:S(2)}) collective-permute-start(bf16[1,512,384]{2,1,0:T(8,128)(2,1)S(1)} %add_convert_fusion.5), channel_id=1, source_target_pairs={{0,6},{2,0},{4,2},{6,4},{1,7},{3,1},{5,3},{7,5},{8,14},{10,8},{12,... | collective-permute-start | bytes 1179656 | tf_op jit(solution)/shard_map/ppermute | solution.py:265
  144.0 19.8 %collective-permute-start.11 = (bf16[1,512,384]{2,1,0:T(8,128)(2,1)S(1)}, bf16[1,512,384]{2,1,0:T(8,128)(2,1)S(1)}, u32[]{:S(2)}, u32[]{:S(2)}) collective-permute-start(bf16[1,512,384]{2,1,0:T(8,128)(2,1)S(1)} %add_convert_fusion.7), channel_id=1, source_target_pairs={{0,2},{2,4},{4,6},{6,0},{1,3},{3,5},{5,7},{7,1},{8,10},{10,12},{12... | collective-permute-start | bytes 1179656 | tf_op jit(solution)/shard_map/ppermute | solution.py:265
  165.1 35.6 %all-to-all-start.1 = ((bf16[64,16,384]{2,1,0:T(8,128)(2,1)}), bf16[64,16,384]{2,1,0:T(8,128)(2,1)S(1)}, u32[]{:S(2)}, u32[]{:S(2)}) async-start(bf16[64,16,384]{2,1,0:T(8,128)(2,1)} %bitcast.15), calls=%async_computation.1 | async-start | bytes 1572864 | tf_op jit(solution)/shard_map/all_to_all | solution.py:291
  173.1 18.6 %collective-permute-start.24 = (bf16[1,512,384]{2,1,0:T(8,128)(2,1)S(1)}, bf16[1,512,384]{2,1,0:T(8,128)(2,1)S(1)}, u32[]{:S(2)}, u32[]{:S(2)}) collective-permute-start(bf16[1,512,384]{2,1,0:T(8,128)(2,1)S(1)} %copy-done.19), channel_id=1, source_target_pairs={{0,2},{2,4},{4,6},{6,0},{1,3},{3,5},{5,7},{7,1},{8,10},{10,12},{12... | collective-permute-start | bytes 1179656 | tf_op jit(solution)/shard_map/ppermute | solution.py:265
  200.8 35.1 %all-to-all-start.3 = ((bf16[64,16,384]{2,1,0:T(8,128)(2,1)}), bf16[64,16,384]{2,1,0:T(8,128)(2,1)S(1)}, u32[]{:S(2)}, u32[]{:S(2)}) async-start(bf16[64,16,384]{2,1,0:T(8,128)(2,1)} %bitcast.22), calls=%async_computation.3 | async-start | bytes 1572864 | tf_op jit(solution)/shard_map/all_to_all | solution.py:291
  (28 other events, 350.1 us)
